TPU v7x, 64 devices: a 2x2x8 block of a 4x4x8 slice. The times are simulated.
64 devices in a mesh: data: 4 (over x, y), cp: 16 (over z, core).
Axes of the slice: x: 2, y: 2, z: 8, core: 2. Of those that a mesh axis runs over, the one named last changes fastest.
The devices are a block of a 4x4x8 slice.
Arguments:
- x_new: bfloat16 [32768, 1536], P(('data', 'cp')), parts along dimension 0
- pos_new: int32 [32768], P(('data', 'cp')), parts along dimension 0
- k_cache: bfloat16 [262144, 2, 128], P(('data', 'cp')), parts along dimension 0
- v_cache: bfloat16 [262144, 2, 128], P(('data', 'cp')), parts along dimension 0
- w_q: bfloat16 [1536, 1536], replicated
- w_k: bfloat16 [1536, 256], replicated
- w_v: bfloat16 [1536, 256], replicated
- w_o: bfloat16 [1536, 1536], replicated
Outputs:
- output: bfloat16 [32768, 1536], P(('data', 'cp')), parts along dimension 0
There are 4 independent parts. A program takes and returns all parts, laid end to end along the dimension named above; an argument that names none is the same for every part.
All inputs are finite; a program needn't handle non-finite values.
Results may differ from a plain program's by a relative error of at most 0.0054015.
Values are sent between devices in bfloat16 or wider.
A program may use at most 768 MiB of HBM per device.

v0:
```python
import math
import jax
import jax.numpy as jnp
from jax import lax
from jax.sharding import PartitionSpec as P

ROPE_BASE = 500000.0
SCORE_BUDGET = 2 ** 26


def rotary(values, positions):
    head_dim = values.shape[-1]
    half_dim = head_dim // 2
    inv_freq = jnp.power(jnp.float32(ROPE_BASE), -(jnp.arange(half_dim, dtype=jnp.float32) * 2.0 / head_dim))
    angles = positions.astype(jnp.float32)[:, None] * inv_freq[None, :]
    cos_a = jnp.cos(angles)[:, None, :]
    sin_a = jnp.sin(angles)[:, None, :]
    low_half = values[..., :half_dim]
    high_half = values[..., half_dim:]
    return jnp.concatenate([low_half * cos_a - high_half * sin_a, high_half * cos_a + low_half * sin_a], axis=-1)


def block_rows(tok_count, row_bytes):
    blk_rows = tok_count
    while blk_rows % 2 == 0 and blk_rows > 8 and blk_rows * row_bytes > SCORE_BUDGET:
        blk_rows = blk_rows // 2
    return blk_rows


def solution(mesh):
    cp_size = mesh.shape["cp"]

    def local_step(x_loc, pos_loc, k_loc, v_loc, w_q, w_k, w_v, w_o):
        tok_dev, model_dim = x_loc.shape
        cache_dev, kv_heads, head_dim = k_loc.shape
        q_heads = w_q.shape[1] // head_dim
        group_size = q_heads // kv_heads
        score_scale = 1.0 / math.sqrt(head_dim)
        q_proj = jnp.dot(x_loc, w_q, preferred_element_type=jnp.float32).astype(jnp.bfloat16)
        k_proj = jnp.dot(x_loc, w_k, preferred_element_type=jnp.float32).astype(jnp.bfloat16)
        v_new = jnp.dot(x_loc, w_v, preferred_element_type=jnp.float32).astype(jnp.bfloat16).reshape(tok_dev, kv_heads, head_dim)
        q_rot = rotary(q_proj.astype(jnp.float32).reshape(tok_dev, q_heads, head_dim), pos_loc).astype(jnp.bfloat16)
        k_new = rotary(k_proj.astype(jnp.float32).reshape(tok_dev, kv_heads, head_dim), pos_loc).astype(jnp.bfloat16)
        keys_all = jnp.concatenate([k_loc, k_new], axis=0)
        vals_all = jnp.concatenate([v_loc, v_new], axis=0)
        key_pos = jnp.concatenate([jnp.full((cache_dev,), -1, jnp.int32), pos_loc])
        q_all = lax.all_gather(q_rot, "cp", axis=0, tiled=True)
        pos_all = lax.all_gather(pos_loc, "cp", axis=0, tiled=True)
        blk_rows = block_rows(tok_dev, q_heads * (cache_dev + tok_dev) * 4)
        n_sub = tok_dev // blk_rows
        q_blocks = q_all.reshape(cp_size * n_sub, blk_rows, kv_heads, group_size, head_dim)
        pos_blocks = pos_all.reshape(cp_size * n_sub, blk_rows)

        def attend(block_args):
            q_blk, q_pos = block_args
            scores = jnp.einsum("qkgd,ckd->kqgc", q_blk, keys_all, preferred_element_type=jnp.float32) * score_scale
            visible = key_pos[None, :] <= q_pos[:, None]
            scores = jnp.where(visible[None, :, None, :], scores, -jnp.inf)
            row_max = jnp.max(scores, axis=-1)
            exp_scores = jnp.exp(scores - row_max[..., None])
            row_sum = jnp.sum(exp_scores, axis=-1)
            weighted = jnp.einsum("kqgc,ckd->kqgd", exp_scores.astype(jnp.bfloat16), vals_all, preferred_element_type=jnp.float32)
            return jnp.stack([row_max, row_sum], axis=-1), weighted

        stats, weighted = lax.map(attend, (q_blocks, pos_blocks))
        stats = stats.reshape(cp_size, n_sub, kv_heads, blk_rows, group_size, 2)
        weighted = weighted.reshape(cp_size, n_sub, kv_heads, blk_rows, group_size, head_dim)
        stats = lax.all_to_all(stats, "cp", 0, 0)
        weighted = lax.all_to_all(weighted, "cp", 0, 0)
        glob_max = jnp.max(stats[..., 0], axis=0)
        factors = jnp.exp(stats[..., 0] - glob_max[None])
        denom_sum = jnp.sum(factors * stats[..., 1], axis=0)
        attn_out = (jnp.sum(factors[..., None] * weighted, axis=0) / denom_sum[..., None]).astype(jnp.bfloat16)
        w_out = w_o.reshape(kv_heads, group_size, head_dim, model_dim)
        proj_out = jnp.einsum("skrgd,kgde->sre", attn_out, w_out, preferred_element_type=jnp.float32).reshape(tok_dev, model_dim)
        return (x_loc.astype(jnp.float32) + proj_out).astype(jnp.bfloat16)

    tok_spec = P(("data", "cp"), None)
    pos_spec = P(("data", "cp"))
    cache_spec = P(("data", "cp"), None, None)
    return jax.shard_map(local_step, mesh=mesh, in_specs=(tok_spec, pos_spec, cache_spec, cache_spec, P(), P(), P(), P()), out_specs=tok_spec, check_vma=False)
```

profile of v0, /device:TPU:22, one launch (start us, length us, event | category | flops | bytes accessed | tf_op | source)
XLA Modules:
  0.0 3468.0 jit_solution(2184430343804598360)
XLA Ops:
  59.2 98.7 %all-gather.3.cloned.1.call-done = bf16[8192,12,128]{0,2,1:T(8,128)(2,1)} async-done(((bf16[512,12,128]{0,2,1:T(8,128)(2,1)}), bf16[8192,12,128]{0,2,1:T(8,128)(2,1)}) %all-gather.3.cloned.1.call-update) | async-done | bytes 25165840 | tf_op jit(solution)/shard_map/all_gather | solution.py:47
  157.8 32.5 copy.42
  190.4 2096.7 %while.12 = (s32[]{:T(128)}, f32[32,2,256,6,2]{2,4,3,1,0:T(2,128)S(1)}, f32[32,2,256,6,128]{4,2,3,1,0:T(8,128)}, s32[4608]{0:T(1024)S(1)}, s32[32,256]{1,0:T(8,1...) while((s32[]{:T(128)}, ...), condition=%wide.region_3.4_spmd, body=%wide.region_0.3_spmd.sunk | while | flops 7404650496 | bytes 181844080 | solution.py:65
  213.4 23.3 bitcast_dynamic-update-slice_fusion.2
  344.4 23.3 bitcast_dynamic-update-slice_fusion.2
  409.9 23.3 bitcast_dynamic-update-slice_fusion.2
  475.4 23.3 bitcast_dynamic-update-slice_fusion.2
  540.9 23.4 bitcast_dynamic-update-slice_fusion.2
  606.5 23.3 bitcast_dynamic-update-slice_fusion.2
  672.0 23.3 bitcast_dynamic-update-slice_fusion.2
  868.6 23.3 bitcast_dynamic-update-slice_fusion.2
  934.1 23.4 bitcast_dynamic-update-slice_fusion.2
  999.6 23.3 bitcast_dynamic-update-slice_fusion.2
  1065.1 23.3 bitcast_dynamic-update-slice_fusion.2
  1130.7 23.3 bitcast_dynamic-update-slice_fusion.2
  1261.7 23.3 bitcast_dynamic-update-slice_fusion.2
  1327.2 23.4 bitcast_dynamic-update-slice_fusion.2
  1392.8 23.3 bitcast_dynamic-update-slice_fusion.2
  1458.3 23.3 bitcast_dynamic-update-slice_fusion.2
  1523.8 23.3 bitcast_dynamic-update-slice_fusion.2
  1589.3 23.3 bitcast_dynamic-update-slice_fusion.2
  1654.9 23.3 bitcast_dynamic-update-slice_fusion.2
  1720.4 23.3 bitcast_dynamic-update-slice_fusion.2
  1785.9 23.3 bitcast_dynamic-update-slice_fusion.2
  1851.4 23.3 bitcast_dynamic-update-slice_fusion.2
  1916.9 23.3 bitcast_dynamic-update-slice_fusion.2
  1982.4 23.3 bitcast_dynamic-update-slice_fusion.2
  2113.5 23.3 bitcast_dynamic-update-slice_fusion.2
  2179.0 23.3 bitcast_dynamic-update-slice_fusion.2
  2244.5 23.3 bitcast_dynamic-update-slice_fusion.2
  2287.0 26.7 all_to_all.10
  2322.5 1110.9 %all-to-all-done.1 = f32[16,2,2,256,6,128]{5,3,4,2,1,0:T(8,128)} async-done(((f32[16,2,2,256,6,128]{5,3,4,2,1,0:T(8,128)}), f32[16,2,2,256,6,128]{5,3,4,2,1,0:T(8,128)}, u32[]{:S(2)}, u32[]{:S(2)}) %all-to-all-start.1) | async-done | bytes 50331680 | tf_op jit(solution)/shard_map/all_to_all | solution.py:69
  (251 shorter events, 1554.0 us)
Async XLA Ops:
  6.5 17.4 copy-start
  6.6 151.3 %all-gather.3.cloned.1.call-start = ((), (), s32[]{:S(2)}) async-start(), calls=%async_computation.2 | async-start | bytes 26738688 | tf_op jit(solution)/shard_map/all_gather | solution.py:47
  20.9 3.1 copy-start.5
  26.9 3.4 copy-start.6
  27.0 3.4 copy-start.8
  27.0 5.8 copy-start.4
  54.8 1.7 copy-start.2
  59.2 131.2 %copy-start.3 = (f32[32,2,256,6,2]{2,4,3,1,0:T(2,128)S(1)}, f32[32,2,256,6,2]{2,4,3,1,0:T(2,128)}, u32[]{:S(2)}) copy-start(f32[32,2,256,6,2]{2,4,3,1,0:T(2,128)} %custom-call) | copy-start | bytes 2359300
  2313.8 1119.6 %all-to-all-start.1 = ((f32[16,2,2,256,6,128]{5,3,4,2,1,0:T(8,128)}), f32[16,2,2,256,6,128]{5,3,4,2,1,0:T(8,128)}, u32[]{:S(2)}, u32[]{:S(2)}) async-start(f32[16,2,2,256,6,128]{5,3,4,2,1,0:T(8,128)} %bitcast.88), calls=%async_computation.1 | async-start | bytes 100663296 | tf_op jit(solution)/shard_map/all_to_all | solution.py:69
  3452.3 2.6 copy-start.7
  3454.9 6.2 copy-start.1
Sparse Core Ops, SparseCore 0:
  22.4 135.3 all-gather.2
where the time goes:
time: 3510 us; the launch traced here: 3470 us
  matrix products  1480 us (42%)
  waiting for transfers between devices  1210 us (34%)
  other arithmetic  665 us (19%)
  blocking collectives  48.6 us (1%)
  local copies, waits for them, and re-layouts  46.8 us (1%)
    all_to_all x1, waiting for transfers between devices, local_step(): weighted = lax.all_to_all(weighted, 'cp', 0, 0)  1110 us
    dot_general x32, matrix products, attend(): jnp.einsum('kqgc,ckd->kqgd', exp_scores.astype(jnp.bfloat16), vals_all, p...  746 us
    dot_general x32, matrix products, attend(): jnp.einsum('qkgd,ckd->kqgc', q_blk, keys_all, preferred_element_type=jnp....  714 us
    reduce_sum x32, other arithmetic, attend(): row_sum = jnp.sum(exp_scores, axis=-1)  612 us
    all_gather x1, waiting for transfers between devices, local_step(): q_all = lax.all_gather(q_rot, 'cp', axis=0, tiled=True)  98.7 us
  transfers between devices with their start and end apart: 2, of which 2 were waited for; matrix products, arithmetic and copies ran while one was open for 0% of the time, Pallas kernels for 0%

commit v1 on v0

v1 whole, which is shorter than its diff:
```python
import functools
import math
import jax
import jax.numpy as jnp
from jax import lax
from jax.experimental import pallas as pl
from jax.experimental.pallas import tpu as pltpu
from jax.sharding import PartitionSpec as P

ROPE_BASE = 500000.0
BLK = 256
HBM = pltpu.HBM
VMEM = pltpu.VMEM
BF16 = jnp.bfloat16
F32 = jnp.float32
MESH_ID = pl.DeviceIdType.MESH
NEG = -1e30
LAG = 2


class Ring:
    def __init__(self, n):
        self.n = n
        me = lax.axis_index("cp")
        self.me = me
        self.sib = me + 1 - 2 * lax.rem(me, 2)
        self.right = lax.rem(me + 2, n)
        self.left = lax.rem(me + n - 2, n)
        self.hops = n // 4
        self.rounds = 4 * (self.hops - 1) + 2
        self.phases = 8 + 4 * self.rounds

    def round_of(self, p):
        return (p - 8) // 4 + 1, lax.rem(p - 8, 4)

    def left_piece(self, base, r):
        s = (r - 1) // 4 + 1
        return lax.rem(base + self.n - 2 * s, self.n), lax.rem(r - 1, 4)

    def right_piece(self, base, r):
        s = (r - 1) // 4 + 1
        return lax.rem(base + 2 * s, self.n), lax.rem(r + 1, 4)

    def piece(self, p):
        r, i = self.round_of(jnp.maximum(p, 8))
        base = jnp.where(i >= 2, self.sib, self.me)
        s = (r - 1) // 4 + 1
        from_right = lax.rem(i, 2)
        dev = lax.rem(base + self.n + (2 * from_right - 1) * 2 * s, self.n)
        j = lax.rem(r - 1 + 2 * from_right, 4)
        early_dev = jnp.where(p >= 4, self.sib, self.me)
        return jnp.where(p < 8, early_dev, dev), jnp.where(p < 8, lax.rem(p, 4), j)

    def head(self, p):
        return self.piece(p)[1] // 2


def dot(a, b):
    return jnp.dot(a, b, preferred_element_type=F32)


def attend_kernel(n, nsb, pairs, scale2, q_in, k_in, v_in, nk_in, nv_in,
                  acc_out, l_out, k_all, v_all, nk_all, nv_all,
                  q_scr, kslot, vslot, nkslot, nvslot, p_scr, kfirst, ones_scr,
                  recv_sem, right_sem, left_sem, sib_sem, own_sib_sem, nrecv_sem, nsend_sem, load_sem, misc_sem, nload_sem):
    ring = Ring(n)
    me, sib, right, left, hops = ring.me, ring.sib, ring.right, ring.left, ring.hops
    rounds, phases = ring.rounds, ring.phases
    tiles = q_scr.shape[0]
    head_tiles = tiles // 2

    def const(value):
        return 0 * me + value

    def send(src, dst, send_sem, recv, to):
        return pltpu.make_async_remote_copy(src_ref=src, dst_ref=dst, send_sem=send_sem, recv_sem=recv,
                                            device_id={"cp": to}, device_id_type=MESH_ID)

    def send_piece(from_own, dev, j, pair_sem, phase, to):
        ksrc = k_in.at[j] if from_own else k_all.at[dev, j]
        vsrc = v_in.at[j] if from_own else v_all.at[dev, j]
        return (send(ksrc, k_all.at[dev, j], pair_sem.at[0], recv_sem.at[phase - 4, 0], to),
                send(vsrc, v_all.at[dev, j], pair_sem.at[1], recv_sem.at[phase - 4, 1], to))

    def send_new(from_own, dev, lo, num, idx, ridx, to):
        ksrc = (nk_in if from_own else nk_all.at[dev]).at[pl.ds(lo, num)]
        vsrc = (nv_in if from_own else nv_all.at[dev]).at[pl.ds(lo, num)]
        return (send(ksrc, nk_all.at[dev, pl.ds(lo, num)], nsend_sem.at[idx, 0], nrecv_sem.at[ridx, 0], to),
                send(vsrc, nv_all.at[dev, pl.ds(lo, num)], nsend_sem.at[idx, 1], nrecv_sem.at[ridx, 1], to))

    def start(copies):
        for c in copies:
            c.start()

    def recv_wait(phase, dev, j):
        for c in send_piece(False, dev, j, right_sem.at[0], phase, me):
            c.wait_recv()

    def nleft(s):
        return lax.rem(me + n - 2 * s, n)

    def nright(s):
        return lax.rem(me + 2 * s, n)

    def nwait(s, side, from_sib):
        base = sib if from_sib else me
        dev = lax.rem(base + (2 * s if side else n - 2 * s), n)
        lo, num = (0, 4) if s < hops else (2 * side, 2)
        for c in send_new(False, dev, lo, num, 0, 2 * (s - 1) + side + (2 * hops if from_sib else 0), me):
            c.wait_recv()

    nsends = []

    def new_step(s):
        for side in (0, 1):
            nwait(s, side, False)
        for side in (0, 1):
            dev = nright(s) if side else nleft(s)
            if s < hops:
                lo, num = (0, 4) if s + 1 < hops else (2 * side, 2)
                idx = len(nsends)
                copies = send_new(False, dev, lo, num, idx, 2 * s + side, left if side else right)
                start(copies)
                nsends.append(num)
            lo, num = (0, 4) if s < hops else (2 * side, 2)
            idx = len(nsends)
            copies = send_new(False, dev, lo, num, idx, 2 * hops + 2 * (s - 1) + side, sib)
            start(copies)
            nsends.append(num)

    barrier = pltpu.get_barrier_semaphore()
    for other in (left, right, sib):
        pl.semaphore_signal(barrier, inc=1, device_id={"cp": other}, device_id_type=MESH_ID)
    pl.semaphore_wait(barrier, 3)

    for other, ridx in ((right, 0), (left, 1), (sib, 4 * hops)):
        start(send_new(True, me, 0, 4, len(nsends), ridx, other))
        nsends.append(4)
    for slot in (1, 2, 3):
        start(send_piece(True, me, slot - 1, right_sem.at[slot % 4], 8 + 4 * (slot - 1), right))
        start(send_piece(True, me, (slot + 1) % 4, left_sem.at[slot % 4], 8 + 4 * (slot - 1) + 1, left))
    for j in range(4):
        start(send_piece(True, me, j, own_sib_sem.at[j], 4 + j, sib))

    def load_piece(own, p, dev, j):
        ksrc = k_in.at[j] if own else k_all.at[dev, j]
        vsrc = v_in.at[j] if own else v_all.at[dev, j]
        slot = lax.rem(p, 4)
        return (pltpu.make_async_copy(ksrc, kslot.at[slot], load_sem.at[slot, 0]),
                pltpu.make_async_copy(vsrc, vslot.at[slot], load_sem.at[slot, 1]))

    first = [pltpu.make_async_copy(q_in, q_scr.at[:, pl.ds(0, BLK // 2)], misc_sem.at[0])]
    first += [pltpu.make_async_copy(k_in.at[2 * h, 0], kfirst.at[h], misc_sem.at[1 + h]) for h in (0, 1)]
    start(first)
    start(load_piece(True, const(0), me, 0))

    ones_scr[...] = jnp.where(lax.broadcasted_iota(jnp.int32, ones_scr.shape, 1) == 0, 1.0, 0.0).astype(BF16)

    def clear(t, _):
        q_scr[t, pl.ds(BLK // 2, BLK // 2)] = jnp.zeros((BLK // 2, BLK), BF16)
        acc_out[t] = jnp.zeros(acc_out.shape[1:], F32)
        l_out[t] = jnp.zeros(l_out.shape[1:], F32)
        return 0
    lax.fori_loop(0, tiles, clear, 0)
    for c in first:
        c.wait()

    def lhs_keys(keys):
        ones = ones_scr[...]
        return jnp.concatenate([keys, jnp.concatenate([ones] * (BLK // 16), axis=0)], axis=1)

    def attend(blocks):
        def scores(b):
            lhs = lhs_keys(b[1]())
            return [dot(lhs, q_scr[b[0] + x]) for x in (0, 1)]

        ahead = scores(blocks[0])
        sums, out = [None, None], [None, None]
        for i in range(len(blocks) + LAG):
            now = ahead
            if i + 1 < len(blocks):
                ahead = scores(blocks[i + 1])
            if i < len(blocks):
                t, _, _, bias, first, last = blocks[i]
                for x in (0, 1):
                    s = now[x] * scale2
                    e = jnp.exp2(s if bias is None else jnp.where(bias, s, NEG))
                    p_scr[x, i % 4] = e.astype(BF16)
                    part = e.reshape(BLK // 8, 8, BLK).sum(axis=0)
                    sums[x] = part if first else sums[x] + part
                    if last:
                        l_out[t + x] = l_out[t + x] + sums[x]
            if i >= LAG:
                t, _, values, _, first, last = blocks[i - LAG]
                v = values()
                for x in (0, 1):
                    part = dot(v, p_scr[x, (i - LAG) % 4])
                    out[x] = part if first else out[x] + part
                    if last:
                        acc_out[t + x] = acc_out[t + x] + out[x]

    def reference_point(i, _):
        lhs = lhs_keys(kfirst[i // 2])
        rows = lax.broadcasted_iota(jnp.int32, (16, BLK), 0)
        for t in range(pairs):
            top = jnp.max(dot(lhs, q_scr[i * pairs + t]), axis=0, keepdims=True)
            q_scr[i * pairs + t, pl.ds(BLK // 2, 16)] = jnp.where(rows == 0, -top, 0.0).astype(BF16)
        return 0
    lax.fori_loop(0, tiles // pairs, reference_point, 0)

    def get_ready(p):
        dev, j = ring.piece(p)

        @pl.when(p < 4)
        def _():
            start(load_piece(True, p, me, j))

        @pl.when(p >= 4)
        def _():
            recv_wait(p, dev, j)
            start(load_piece(False, p, dev, j))
        r, i = ring.round_of(jnp.maximum(p, 8))

        for s, at in new_steps:
            @pl.when(p == at)
            def _():
                new_step(s)

        for side in (0, 1):
            @pl.when((p >= 8) & (i == side))
            def _():
                sem = sib_sem.at[side, lax.rem(r, 2)]

                @pl.when(r > 2)
                def _():
                    for c in send_piece(False, dev, j, sem, p + 2, sib):
                        c.wait_send()
                start(send_piece(False, dev, j, sem, p + 2, sib))
                pool, to = (left_sem, left) if side else (right_sem, right)
                slot = r + 3
                pair_sem = pool.at[lax.rem(slot, 4)]
                phase = 8 + 4 * (slot - 1) + side

                @pl.when(r == 1)
                def _():
                    start(send_piece(True, me, 1 if side else 3, pair_sem, phase, to))

                @pl.when((r > 1) & (slot <= rounds))
                def _():
                    odev, oj = (ring.right_piece if side else ring.left_piece)(me, r - 1)
                    copies = send_piece(False, odev, oj, pair_sem, phase, to)
                    for c in copies:
                        c.wait_send()
                    start(copies)

    def run_phase(p, _):
        dev, j = ring.piece(p)
        for c in load_piece(False, p, dev, j):
            c.wait()

        @pl.when(p + 1 < phases)
        def _():
            get_ready(p + 1)

        @pl.when(p == new_at)
        def _():
            run_new()
        slot = lax.rem(p, 4)
        t0 = (j // 2) * head_tiles
        attend([(t0 + 2 * u, lambda k=k: kslot[slot, k], lambda k=k: vslot[slot, k], None, k == 0, k == nsb - 1)
                for u in range(pairs) for k in range(nsb)])
        return 0

    def run_new():
        for s in range(1, hops + 1):
            for side in (0, 1):
                nwait(s, side, True)
        for c in send_new(False, sib, 0, 4, 0, 4 * hops, me):
            c.wait_recv()

        def loads(d):
            dev = lax.rem(me + d, n)
            return (pltpu.make_async_copy(nk_all.at[dev], nkslot.at[dev], nload_sem.at[d, 0]),
                    pltpu.make_async_copy(nv_all.at[dev], nvslot.at[dev], nload_sem.at[d, 1]))

        def start_loads(d, _):
            start(loads(d))
            return 0

        def wait_loads(d, _):
            for c in loads(d):
                c.wait()
            return 0
        start((pltpu.make_async_copy(nk_in, nkslot.at[me], nload_sem.at[0, 0]),
               pltpu.make_async_copy(nv_in, nvslot.at[me], nload_sem.at[0, 1])))
        lax.fori_loop(1, n, start_loads, 0)
        lax.fori_loop(0, n, wait_loads, 0)
        groups_lo = me // 4 + 1
        groups = n // 2 + 1
        rowcol = (lax.broadcasted_iota(jnp.int32, (BLK, BLK), 0) - lax.broadcasted_iota(jnp.int32, (BLK, BLK), 1))

        def group(u, _):
            h, grp = u // groups, lax.rem(u, groups)
            upper = (grp >= groups_lo).astype(jnp.int32)
            t0 = h * head_tiles + upper * (head_tiles // 2)
            own = jnp.where(upper == 1, 2 * n - 1 - me, me)
            block0 = 4 * jnp.where(upper == 1, grp - groups_lo, grp)
            blocks = []
            for trio in range(pairs // 2):
                for k in range(4):
                    block = block0 + k
                    at = jnp.where(block < n, block, 2 * n - 1 - block)
                    i = 2 * h + (block >= n).astype(jnp.int32)
                    blocks.append((t0 + 2 * trio, lambda at=at, i=i: nkslot[at, i], lambda at=at, i=i: nvslot[at, i],
                                   rowcol <= (own - block) * BLK, k == 0, k == 3))
            attend(blocks)
            return 0
        lax.fori_loop(0, 2 * groups, group, 0)

    new_at = 8 + 4 * (rounds - 4)
    new_steps = [(1, 3), (2, 16), (3, 28), (4, 40)] if hops == 4 else [(s + 1, 3 + s) for s in range(hops)]
    lax.fori_loop(0, phases, run_phase, 0)

    for idx, num in enumerate(nsends):
        for c in send_new(True, me, 0, num, idx, 0, me):
            c.wait_send()
    for slot in range(rounds - 3, rounds + 1):
        for pool in (right_sem, left_sem):
            for c in send_piece(True, me, 0, pool.at[slot % 4], 4, me):
                c.wait_send()
    for side in (0, 1):
        for r in (rounds - 1, rounds):
            for c in send_piece(True, me, 0, sib_sem.at[side, r % 2], 4, me):
                c.wait_send()
    for j in range(4):
        for c in send_piece(True, me, j, own_sib_sem.at[j], 4, me):
            c.wait_send()


def guard_kernel(n, nsb, scale, q_ref, acc_ref, l_ref, k_in, v_in, nk_in, nv_in, k_all, v_all, nk_all, nv_all,
                 o_ref, kbuf, vbuf, m_scr, l_scr, acc_scr, sem):
    me = lax.axis_index("cp")
    tiles = q_ref.shape[0]
    head_tiles = tiles // 2

    def tile(t, _):
        denom = jnp.sum(l_ref[t], axis=0, keepdims=True)
        acc = acc_ref[t]
        fine = (jnp.abs(acc) < jnp.inf) & (denom > 2.0 ** -60) & (denom < 2.0 ** 100)
        o_ref[t] = (acc / denom).astype(BF16)
        faults = jnp.sum(jnp.where(fine, 0.0, 1.0))

        @pl.when(faults > 0.0)
        def _():
            h = t // head_tiles
            upper = lax.rem(t, head_tiles) // (head_tiles // 2)
            own = jnp.where(upper == 1, 2 * n - 1 - me, me)
            m_scr[...] = jnp.full(m_scr.shape, NEG, F32)
            l_scr[...] = jnp.zeros_like(l_scr)
            acc_scr[...] = jnp.zeros_like(acc_scr)

            def fetch(k_src, v_src):
                copies = (pltpu.make_async_copy(k_src, kbuf, sem.at[0]), pltpu.make_async_copy(v_src, vbuf, sem.at[1]))
                for c in copies:
                    c.start()
                for c in copies:
                    c.wait()

            def step(limit):
                s = jnp.dot(kbuf[...], q_ref[t], preferred_element_type=F32) * scale
                rows = lax.broadcasted_iota(jnp.int32, s.shape, 0) - lax.broadcasted_iota(jnp.int32, s.shape, 1)
                seen = rows <= limit
                s = jnp.where(seen, s, -jnp.inf)
                m_old = m_scr[...]
                m_new = jnp.maximum(m_old, jnp.max(s, axis=0, keepdims=True))
                e = jnp.exp(s - m_new)
                old = jnp.exp(m_old - m_new)
                m_scr[...] = m_new
                l_scr[...] = l_scr[...] * old + jnp.sum(e, axis=0, keepdims=True)
                acc_scr[...] = acc_scr[...] * old + jnp.dot(vbuf[...], e.astype(BF16), preferred_element_type=F32)

            def cached(b, _):
                dev, rem = b // (2 * nsb), lax.rem(b, 2 * nsb)
                j, k = 2 * h + rem // nsb, lax.rem(rem, nsb)

                @pl.when(dev == me)
                def _():
                    fetch(k_in.at[j, k], v_in.at[j, k])

                @pl.when(dev != me)
                def _():
                    fetch(k_all.at[dev, j, k], v_all.at[dev, j, k])
                step(0 * me + BLK)
                return 0

            def new(b, _):
                dev = jnp.where(b < n, b, 2 * n - 1 - b)
                j = 2 * h + (b >= n).astype(jnp.int32)

                @pl.when(dev == me)
                def _():
                    fetch(nk_in.at[j], nv_in.at[j])

                @pl.when(dev != me)
                def _():
                    fetch(nk_all.at[dev, j], nv_all.at[dev, j])
                step((own - b) * BLK)
                return 0
            lax.fori_loop(0, 2 * nsb * n, cached, 0)
            lax.fori_loop(0, own + 1, new, 0)
            o_ref[t] = (acc_scr[...] / l_scr[...]).astype(BF16)
        return 0
    lax.fori_loop(0, tiles, tile, 0)


def rotate(low, high, cos_a, sin_a):
    return low * cos_a - high * sin_a, high * cos_a + low * sin_a


def solution(mesh):
    n = mesh.shape["cp"]

    def local_step(x_loc, pos_loc, k_loc, v_loc, w_q, w_k, w_v, w_o):
        tok_dev, model_dim = x_loc.shape
        cache_dev, kv_heads, head_dim = k_loc.shape
        q_heads = w_q.shape[1] // head_dim
        group = q_heads // kv_heads
        half = head_dim // 2
        nsb = cache_dev // (2 * BLK)
        pairs = group
        tiles = 2 * q_heads
        inv_freq = jnp.power(jnp.float32(ROPE_BASE), -(jnp.arange(half, dtype=F32) * 2.0 / head_dim))
        angles = inv_freq[:, None] * pos_loc.astype(F32)[None, :]
        cos_t, sin_t = jnp.cos(angles), jnp.sin(angles)

        k_pieces = jnp.transpose(k_loc, (1, 0, 2)).reshape(4, nsb, BLK, head_dim)
        v_pieces = jnp.transpose(v_loc.reshape(2, nsb, BLK, kv_heads, head_dim), (3, 0, 1, 4, 2)).reshape(4, nsb, head_dim, BLK)

        q_t = lax.dot_general(w_q, x_loc, (((0,), (1,)), ((), ())), preferred_element_type=F32).astype(BF16).astype(F32)
        q_t = q_t.reshape(q_heads, head_dim, tok_dev)
        low, high = rotate(q_t[:, :half], q_t[:, half:], cos_t[None], sin_t[None])
        q_t = jnp.concatenate([low, high], axis=1).astype(BF16)
        q_tiles = jnp.transpose(q_t.reshape(kv_heads, group, head_dim, 2, BLK), (0, 3, 1, 2, 4)).reshape(tiles, head_dim, BLK)

        k_new = jnp.dot(x_loc, w_k, preferred_element_type=F32).astype(BF16).astype(F32).reshape(tok_dev, kv_heads, head_dim)
        low, high = rotate(k_new[..., :half], k_new[..., half:], cos_t.T[:, None, :], sin_t.T[:, None, :])
        k_new = jnp.concatenate([low, high], axis=-1).astype(BF16)
        nk = jnp.transpose(k_new, (1, 0, 2)).reshape(4, BLK, head_dim)
        v_new = lax.dot_general(w_v, x_loc, (((0,), (1,)), ((), ())), preferred_element_type=F32).astype(BF16)
        nv = jnp.transpose(v_new.reshape(kv_heads, head_dim, 2, BLK), (0, 2, 1, 3)).reshape(4, head_dim, BLK)

        hops = n // 4
        rounds = 4 * (hops - 1) + 2
        phases = 8 + 4 * rounds
        any_spec = pl.BlockSpec(memory_space=pl.ANY)
        vmem_spec = pl.BlockSpec(memory_space=VMEM)
        dma = pltpu.SemaphoreType.DMA
        scale2 = math.log2(math.e) / math.sqrt(head_dim)
        n_new_sends = 3 + 2 * (hops - 1) + 2 * hops
        acc, l, k_all, v_all, nk_all, nv_all = pl.pallas_call(
            functools.partial(attend_kernel, n, nsb, pairs, scale2),
            out_shape=(
                jax.ShapeDtypeStruct((tiles, head_dim, BLK), F32),
                jax.ShapeDtypeStruct((tiles, 8, BLK), F32),
                jax.ShapeDtypeStruct((n,) + k_pieces.shape, BF16),
                jax.ShapeDtypeStruct((n,) + v_pieces.shape, BF16),
                jax.ShapeDtypeStruct((n,) + nk.shape, BF16),
                jax.ShapeDtypeStruct((n,) + nv.shape, BF16),
            ),
            in_specs=[any_spec] * 5,
            out_specs=(vmem_spec, vmem_spec, any_spec, any_spec, any_spec, any_spec),
            scratch_shapes=[
                VMEM((tiles, BLK, BLK), BF16),
                VMEM((4, nsb, BLK, head_dim), BF16),
                VMEM((4, nsb, head_dim, BLK), BF16),
                VMEM((n, 4, BLK, head_dim), BF16),
                VMEM((n, 4, head_dim, BLK), BF16),
                VMEM((2, 4, BLK, BLK), BF16),
                VMEM((2, BLK, head_dim), BF16),
                VMEM((16, head_dim), BF16),
                dma((phases - 4, 2)),
                dma((4, 2)),
                dma((4, 2)),
                dma((2, 2, 2)),
                dma((4, 2)),
                dma((4 * hops + 1, 2)),
                dma((n_new_sends, 2)),
                dma((4, 2)),
                dma((3,)),
                dma((n, 2)),
            ],
            compiler_params=pltpu.CompilerParams(collective_id=0, has_side_effects=True, vmem_limit_bytes=56 * 2 ** 20),
            name="ring_attention",
        )(q_tiles, k_pieces, v_pieces, nk, nv)

        o_t = pl.pallas_call(
            functools.partial(guard_kernel, n, nsb, 1.0 / math.sqrt(head_dim)),
            out_shape=jax.ShapeDtypeStruct((tiles, head_dim, BLK), BF16),
            in_specs=[vmem_spec] * 3 + [any_spec] * 8,
            out_specs=vmem_spec,
            scratch_shapes=[VMEM((BLK, head_dim), BF16), VMEM((head_dim, BLK), BF16), VMEM((1, BLK), F32), VMEM((1, BLK), F32),
                            VMEM((head_dim, BLK), F32), dma((2,))],
            compiler_params=pltpu.CompilerParams(vmem_limit_bytes=24 * 2 ** 20),
            name="guard",
        )(q_tiles, acc, l, k_pieces, v_pieces, nk, nv, k_all, v_all, nk_all, nv_all)

        o_t = o_t.reshape(kv_heads, 2, group, head_dim, BLK)
        w_out = w_o.reshape(kv_heads, group, head_dim, model_dim)
        proj = jnp.einsum("kygdt,kgde->yte", o_t, w_out, preferred_element_type=F32).reshape(tok_dev, model_dim)
        return (x_loc.astype(F32) + proj).astype(BF16)

    tok_spec = P(("data", "cp"), None)
    pos_spec = P(("data", "cp"))
    cache_spec = P(("data", "cp"), None, None)
    return jax.shard_map(local_step, mesh=mesh, in_specs=(tok_spec, pos_spec, cache_spec, cache_spec, P(), P(), P(), P()), out_specs=tok_spec, check_vma=False)
```

time: 3510 us -> 469 us (0.13); the launches traced: 3470 us -> 469 us
  matrix products: 1480 us -> 13.8 us
  waiting for transfers between devices: 1210 us -> 0 us
  other arithmetic: 665 us -> 6.37 us
  Pallas kernels: 0 us -> 429 us
  blocking collectives: 48.6 us -> 0 us
    dot_general x68 -> x4, matrix products: 1480 us -> 13.8 us  [the longest x1 6.11 us: local_step(): jnp.einsum('kygdt,kgde->yte', o_t, w_out, preferred_element_type=F32)]
    all_to_all x1 -> x0, waiting for transfers between devices: 1110 us -> none  [local_step(): weighted = lax.all_to_all(weighted, 'cp', 0, 0)]
    reduce_sum x34 -> x0, other arithmetic: 631 us -> none  [the longest x32 612 us: attend(): row_sum = jnp.sum(exp_scores, axis=-1)]
    pallas_call x0 -> x2, Pallas kernels: none -> 429 us  [the longest x1 424 us: local_step(): pl.pallas_call(functools.partial(attend_kernel, n, nsb, pairs, scale2), o...]
    all_gather x1 -> x0, waiting for transfers between devices: 98.7 us -> none  [local_step(): q_all = lax.all_gather(q_rot, 'cp', axis=0, tiled=True)]
  transfers between devices with their start and end apart: 2 -> 0, of which waited for: 2 -> 0; matrix products, arithmetic and copies ran while one was open for 0% -> 0% of each run, Pallas kernels for 0% -> 0%
where the time goes in v1:
time: 469 us
  Pallas kernels  429 us (91%)
  local copies, waits for them, and re-layouts  19.5 us (4%)
  matrix products  13.8 us (3%)
  other arithmetic  6.37 us (1%)
    pallas_call x1, Pallas kernels, local_step(): pl.pallas_call(functools.partial(attend_kernel, n, nsb, pairs, scale2), o...  424 us
    unnamed x34, local copies, waits for them, and re-layouts  9.72 us

profile of v1, /device:TPU:22, one launch (start us, length us, event | category | flops | bytes accessed | tf_op | source)
XLA Modules:
  0.0 468.8 jit_solution(5918331162286448268)
XLA Ops:
  0.0 0.8 convert_element_type.25
  0.9 0.3 copy-done
  1.2 2.0 convolution_convert_fusion.2
  3.2 0.6 convolution_convert_fusion.1
  3.8 0.1 reshape.161
  3.9 0.7 copy.21
  4.7 0.2 copy.26
  4.9 0.5 multiply_cosine_fusion.1
  5.4 1.0 multiply_cosine_fusion
  6.4 0.2 copy.25
  6.6 0.1 subtract_convert_fusion.1
  6.8 0.8 pad_maximum_fusion
  7.6 0.5 copy-done.14
  8.1 5.0 %convolution_convert_fusion = bf16[1536,512]{1,0:T(8,128)(2,1)S(1)} fusion(bf16[1536,1536]{1,0:T(8,128)(2,1)} %param.12, bf16[512,1536]{1,0:T(8,128)(2,1)S(1)} %copy-done.14), kind=kOutput, calls=%fused_computation.5 | convolution fusion | flops 2416705536 | bytes 7864320 | tf_op jit(solution)/shard_map/dot_general | solution.py:439
  13.2 0.4 convert.20
  13.6 0.6 subtract_convert_fusion
  14.2 0.2 concatenate.13
  14.4 0.2 concatenate.14
  14.5 2.0 maximum_bitcast_fusion
  16.6 1.4 copy.16
  18.0 0.7 copy-done.11
  18.7 1.8 copy.17
  20.5 0.6 copy-done.12
  21.1 3.8 copy.18
  24.9 424.5 %ring_attention.1 = (f32[24,128,256]{2,1,0:T(8,128)}, f32[24,8,256]{2,1,0:T(8,128)}, bf16[16,4,8,256,128]{4,3,2,1,0:T(8,128)(2,1)}, bf16[16,4,8,128,256]{4,3,2,1...) custom-call(bf16[24,128,256]{2,1,0:T(8,128)(2,1)} %bitcast.43, ...), custom_call_target="tpu_custom_call" | custom-call | tf_op jit(solution)/shard_map/ring_attention/pallas_call | solution.py:460
  449.5 2.2 copy-done.5
  451.6 2.2 copy-done.6
  453.8 1.9 copy-done.7
  455.7 0.9 copy-done.10
  456.6 4.4 guard.1
  461.1 1.6 copy.22
  462.7 6.1 %fusion.8 = bf16[512,1536]{1,0:T(8,128)(2,1)} fusion(bf16[512,128,6,2]{1,0,3,2:T(8,128)(2,1)} %bitcast.52, bf16[2,6,128,1536]{3,2,1,0:T(8,128)(2,1)} %bitcast.55, bf16[512,1536]{1,0:T(8,128)(2,1)} %param.8), kind=kOutput, calls=%fused_computation.4 | convolution fusion | flops 2418278400 | bytes 9437184 | tf_op jit(solution)/shard_map/kygdt,kgde->yte/dot_general | solution.py:509
  (26 shorter events, 0.1 us)
Async XLA Ops:
  0.0 1.1 copy-start
  0.0 3.2 copy-start.13
  0.0 3.2 copy-start.15
  6.6 1.5 copy-start.14
  16.6 2.2 copy-start.11
  18.7 2.3 copy-start.12
  24.9 424.5 %copy-start.2 = (bf16[2,4096,128]{2,1,0:T(8,128)(2,1)S(1)}, bf16[2,4096,128]{2,1,0:T(8,128)(2,1)}, u32[]{:S(2)}) copy-start(bf16[2,4096,128]{2,1,0:T(8,128)(2,1)} %copy.17) | copy-start | bytes 6291460
  24.9 424.5 %copy-start.3 = (bf16[2,8,256,2,128]{2,4,1,0,3:T(8,128)(2,1)S(1)}, bf16[2,8,256,2,128]{2,4,1,0,3:T(8,128)(2,1)}, u32[]{:S(2)}) copy-start(bf16[2,8,256,2,128]{2,4,1,0,3:T(8,128)(2,1)} %copy.18) | copy-start | bytes 6291460
  24.9 424.5 %copy-start.4 = (bf16[2,2,6,128,256]{4,3,2,1,0:T(8,128)(2,1)S(1)}, bf16[2,2,6,128,256]{4,3,2,1,0:T(8,128)(2,1)}, u32[]{:S(2)}) copy-start(bf16[2,2,6,128,256]{4,3,2,1,0:T(8,128)(2,1)} %copy.16) | copy-start | bytes 4718596
  24.9 424.6 %copy-start.8 = (bf16[512,2,128]{2,0,1:T(8,128)(2,1)S(1)}, bf16[512,2,128]{2,0,1:T(8,128)(2,1)}, u32[]{:S(2)}) copy-start(bf16[512,2,128]{2,0,1:T(8,128)(2,1)} %pad_maximum_fusion) | copy-start | bytes 786436
  24.9 424.6 %copy-start.9 = (bf16[2,128,2,256]{3,1,2,0:T(8,128)(2,1)S(1)}, bf16[2,128,2,256]{3,1,2,0:T(8,128)(2,1)}, u32[]{:S(2)}) copy-start(bf16[2,128,2,256]{3,1,2,0:T(8,128)(2,1)} %copy.21) | copy-start | bytes 786436
  449.4 2.2 copy-start.5
  451.6 2.2 copy-start.6
  453.8 1.9 copy-start.7
  455.7 0.9 copy-start.10
  462.7 6.1 %copy-start.1 = (bf16[1536,256]{1,0:T(8,128)(2,1)S(1)}, bf16[1536,256]{1,0:T(8,128)(2,1)}, u32[]{:S(2)}) copy-start(bf16[1536,256]{1,0:T(8,128)(2,1)} %param.13) | copy-start | bytes 2359300

commit v2 on v1

v2 whole, which is shorter than its diff:
```python
import functools
import math
import jax
import jax.numpy as jnp
from jax import lax
from jax.experimental import pallas as pl
from jax.experimental.pallas import tpu as pltpu
from jax.sharding import PartitionSpec as P

ROPE_BASE = 500000.0
BLK = 256
HBM = pltpu.HBM
VMEM = pltpu.VMEM
BF16 = jnp.bfloat16
F32 = jnp.float32
MESH_ID = pl.DeviceIdType.MESH
NEG = -1e30
SIDES = (0, 1)
LAG = 2


class Ring:
    def __init__(self, n):
        self.n = n
        me = lax.axis_index("cp")
        self.me = me
        self.sib = me + 1 - 2 * lax.rem(me, 2)
        self.right = lax.rem(me + 2, n)
        self.left = lax.rem(me + n - 2, n)
        self.hops = n // 4
        self.rounds = 4 * (self.hops - 1) + 2
        self.phases = 8 + 4 * self.rounds

    def round_of(self, p):
        return (p - 8) // 4 + 1, lax.rem(p - 8, 4)

    def far(self, base, r, side):
        s = (r - 1) // 4 + 1
        return lax.rem(base + self.n + (2 * side - 1) * 2 * s, self.n), lax.rem(r - 1 + 2 * side, 4)

    def piece(self, p):
        r, i = self.round_of(jnp.maximum(p, 8))
        dev, j = self.far(jnp.where(i >= 2, self.sib, self.me), r, lax.rem(i, 2))
        early_dev = jnp.where(p >= 4, self.sib, self.me)
        return jnp.where(p < 8, early_dev, dev), jnp.where(p < 8, lax.rem(p, 4), j)


def dot(a, b):
    return jnp.dot(a, b, preferred_element_type=F32)


def attend_kernel(n, nsb, pairs, scale2, x_in, wq_in, wk_in, wv_in, cos_in, sin_in, k_in, v_in,
                  acc_out, l_out, q_all, k_all, v_all, nk_all, nv_all,
                  q_scr, kslot, vslot, nkslot, nvslot, p_scr, kfirst, ones_scr, x_scr, wq_scr, wkv_scr, cos_scr, sin_scr,
                  recv_sem, way_sem, sib_sem, own_sib_sem, nrecv_sem, nsend_sem, load_sem, misc_sem, nload_sem):
    ring = Ring(n)
    me, sib, right, left, hops = ring.me, ring.sib, ring.right, ring.left, ring.hops
    rounds, phases = ring.rounds, ring.phases
    tiles = q_scr.shape[0]
    head_tiles = tiles // 2

    def const(value):
        return 0 * me + value

    def send(src, dst, send_sem, recv, to):
        return pltpu.make_async_remote_copy(src_ref=src, dst_ref=dst, send_sem=send_sem, recv_sem=recv,
                                            device_id={"cp": to}, device_id_type=MESH_ID)

    def send_piece(from_own, dev, j, pair_sem, phase, to):
        ksrc = k_in.at[j] if from_own else k_all.at[dev, j]
        vsrc = v_in.at[j] if from_own else v_all.at[dev, j]
        return (send(ksrc, k_all.at[dev, j], pair_sem.at[0], recv_sem.at[phase - 4, 0], to),
                send(vsrc, v_all.at[dev, j], pair_sem.at[1], recv_sem.at[phase - 4, 1], to))

    def send_new(from_own, dev, lo, num, idx, ridx, to):
        ksrc = (nkslot if from_own else nk_all).at[dev, pl.ds(lo, num)]
        vsrc = (nvslot if from_own else nv_all).at[dev, pl.ds(lo, num)]
        return (send(ksrc, nk_all.at[dev, pl.ds(lo, num)], nsend_sem.at[idx, 0], nrecv_sem.at[ridx, 0], to),
                send(vsrc, nv_all.at[dev, pl.ds(lo, num)], nsend_sem.at[idx, 1], nrecv_sem.at[ridx, 1], to))

    def start(copies):
        for c in copies:
            c.start()

    def recv_wait(phase, dev, j):
        for c in send_piece(False, dev, j, own_sib_sem.at[0], phase, me):
            c.wait_recv()

    def nleft(s):
        return lax.rem(me + n - 2 * s, n)

    def nright(s):
        return lax.rem(me + 2 * s, n)

    def nwait(s, side, from_sib):
        base = sib if from_sib else me
        dev = lax.rem(base + (2 * s if side else n - 2 * s), n)
        lo, num = (0, 4) if s < hops else (2 * side, 2)
        for c in send_new(False, dev, lo, num, 0, 2 * (s - 1) + side + (2 * hops if from_sib else 0), me):
            c.wait_recv()

    nsends = []

    def new_step(s):
        for side in SIDES:
            nwait(s, side, False)
        for side in SIDES:
            dev = nright(s) if side else nleft(s)
            if s < hops:
                lo, num = (0, 4) if s + 1 < hops else (2 * side, 2)
                idx = len(nsends)
                copies = send_new(False, dev, lo, num, idx, 2 * s + side, left if side else right)
                start(copies)
                nsends.append(num)
            lo, num = (0, 4) if s < hops else (2 * side, 2)
            idx = len(nsends)
            copies = send_new(False, dev, lo, num, idx, 2 * hops + 2 * (s - 1) + side, sib)
            start(copies)
            nsends.append(num)

    barrier = pltpu.get_barrier_semaphore()
    for other in (left, right, sib):
        pl.semaphore_signal(barrier, inc=1, device_id={"cp": other}, device_id_type=MESH_ID)
    pl.semaphore_wait(barrier, 3)

    def own_slot(slot):
        for side in SIDES:
            start(slot_copies(slot, side, True, me, lax.rem(slot - 1 + 2 * side, 4)))

    def slot_copies(slot, side, own, dev, j):
        return send_piece(own, dev, j, way_sem.at[side, lax.rem(slot, 4)], 4 + 4 * slot + side, (right, left)[side])

    own_slot(const(1))
    for j in range(4):
        start(send_piece(True, me, j, own_sib_sem.at[j], 4 + j, sib))

    def load_piece(own, p, dev, j):
        ksrc = k_in.at[j] if own else k_all.at[dev, j]
        vsrc = v_in.at[j] if own else v_all.at[dev, j]
        slot = lax.rem(p, 4)
        return (pltpu.make_async_copy(ksrc, kslot.at[slot], load_sem.at[slot, 0]),
                pltpu.make_async_copy(vsrc, vslot.at[slot], load_sem.at[slot, 1]))

    kv_width = wk_in.shape[1]
    first = [pltpu.make_async_copy(x_in, x_scr, misc_sem.at[0]),
             pltpu.make_async_copy(wk_in, wkv_scr.at[:, pl.ds(0, kv_width)], misc_sem.at[1]),
             pltpu.make_async_copy(wv_in, wkv_scr.at[:, pl.ds(kv_width, kv_width)], misc_sem.at[2]),
             pltpu.make_async_copy(cos_in, cos_scr, misc_sem.at[3]),
             pltpu.make_async_copy(sin_in, sin_scr, misc_sem.at[4])]
    then = [pltpu.make_async_copy(wq_in, wq_scr, misc_sem.at[5])]
    then += [pltpu.make_async_copy(k_in.at[2 * h, 0], kfirst.at[h], misc_sem.at[6 + h]) for h in SIDES]
    start(first)
    start(then)
    start(load_piece(True, const(0), me, 0))

    ones_scr[...] = jnp.where(lax.broadcasted_iota(jnp.int32, ones_scr.shape, 1) == 0, 1.0, 0.0).astype(BF16)

    def clear(t, _):
        q_scr[t, pl.ds(BLK // 2, BLK // 2)] = jnp.zeros((BLK // 2, BLK), BF16)
        acc_out[t] = jnp.zeros(acc_out.shape[1:], F32)
        l_out[t] = jnp.zeros(l_out.shape[1:], F32)
        return 0
    lax.fori_loop(0, tiles, clear, 0)
    for c in first:
        c.wait()

    head_dim = BLK // 2

    def turned(u):
        u = u.astype(BF16).astype(F32)
        return (u * cos_scr[...] + pltpu.roll(u, head_dim // 2, 1) * sin_scr[...]).astype(BF16)

    new_kv = dot(x_scr[...], wkv_scr[...])
    for h in SIDES:
        keys = turned(new_kv[:, h * head_dim:(h + 1) * head_dim])
        values = new_kv[:, kv_width + h * head_dim:kv_width + (h + 1) * head_dim].T.astype(BF16)
        for half in SIDES:
            nkslot[me, 2 * h + half] = keys[half * BLK:(half + 1) * BLK]
            nvslot[me, 2 * h + half] = values[:, half * BLK:(half + 1) * BLK]
    for c in then:
        c.wait()
    heads = 4

    def project(c, _):
        width = heads * head_dim
        z = dot(x_scr[...], wq_scr[:, pl.ds(pl.multiple_of(c * width, width), width)])
        for i in range(heads):
            head = c * heads + i
            t = (head // pairs) * head_tiles + lax.rem(head, pairs)
            u = turned(z[:, i * head_dim:(i + 1) * head_dim]).astype(F32).T.astype(BF16)
            for half in SIDES:
                q_scr[t + half * pairs, pl.ds(0, head_dim)] = u[:, half * BLK:(half + 1) * BLK]
        return 0
    lax.fori_loop(0, tiles // (2 * heads), project, 0)

    for other, ridx in ((right, 0), (left, 1), (sib, 4 * hops)):
        start(send_new(True, me, 0, 4, len(nsends), ridx, other))
        nsends.append(4)
    own_slot(const(2))
    own_slot(const(3))
    kept = [pltpu.make_async_copy(q_scr.at[:, pl.ds(0, head_dim)], q_all, misc_sem.at[8]),
            pltpu.make_async_copy(nkslot.at[me], nk_all.at[me], misc_sem.at[9]),
            pltpu.make_async_copy(nvslot.at[me], nv_all.at[me], misc_sem.at[10])]
    start(kept)

    def lhs_keys(keys):
        ones = ones_scr[...]
        return jnp.concatenate([keys, jnp.concatenate([ones] * (BLK // 16), axis=0)], axis=1)

    def attend(blocks):
        def scores(b):
            lhs = lhs_keys(b[1]())
            return [dot(lhs, q_scr[b[0] + x]) for x in SIDES]

        ahead = scores(blocks[0])
        sums, out = [None, None], [None, None]
        for i in range(len(blocks) + LAG):
            now = ahead
            if i + 1 < len(blocks):
                ahead = scores(blocks[i + 1])
            if i < len(blocks):
                t, _, _, bias, first, last = blocks[i]
                for x in SIDES:
                    s = now[x] * scale2
                    e = jnp.exp2(s if bias is None else jnp.where(bias, s, NEG))
                    p_scr[x, i % 4] = e.astype(BF16)
                    part = e.reshape(BLK // 8, 8, BLK).sum(axis=0)
                    sums[x] = part if first else sums[x] + part
                    if last:
                        l_out[t + x] = l_out[t + x] + sums[x]
            if i >= LAG:
                t, _, values, _, first, last = blocks[i - LAG]
                v = values()
                for x in SIDES:
                    part = dot(v, p_scr[x, (i - LAG) % 4])
                    out[x] = part if first else out[x] + part
                    if last:
                        acc_out[t + x] = acc_out[t + x] + out[x]

    def reference_point(i, _):
        lhs = lhs_keys(kfirst[i // 2])
        rows = lax.broadcasted_iota(jnp.int32, (16, BLK), 0)
        for t in range(pairs):
            top = jnp.max(dot(lhs, q_scr[i * pairs + t]), axis=0, keepdims=True)
            q_scr[i * pairs + t, pl.ds(BLK // 2, 16)] = jnp.where(rows == 0, -top, 0.0).astype(BF16)
        return 0
    lax.fori_loop(0, tiles // pairs, reference_point, 0)

    def get_ready(p):
        dev, j = ring.piece(p)

        @pl.when(p < 4)
        def _():
            start(load_piece(True, p, me, j))

        @pl.when(p >= 4)
        def _():
            recv_wait(p, dev, j)
            start(load_piece(False, p, dev, j))

        for s, at in enumerate(new_steps):
            @pl.when(p == at)
            def _():
                new_step(s + 1)
        for s, at in enumerate(new_parts):
            @pl.when(p == at)
            def _():
                for side in SIDES:
                    nwait(s + 1, side, True)
                if s == 0:
                    for c in send_new(False, sib, 0, 4, 0, 4 * hops, me):
                        c.wait_recv()

        @pl.when(new_part(p) >= 0)
        def _():
            each_load(new_part(p), lambda c: c.start())
        r, i = ring.round_of(jnp.maximum(p, 8))

        @pl.when((p >= 8) & (i < 2))
        def _():
            copies = send_piece(False, dev, j, sib_sem.at[i, lax.rem(r, 2)], p + 2, sib)

            @pl.when(r > 2)
            def _():
                for c in copies:
                    c.wait_send()
            start(copies)

        @pl.when((p >= 8) & (i == 0) & (r > 1) & (r + 2 <= rounds))
        def _():
            @pl.when(r == 2)
            def _():
                own_slot(r + 2)

            @pl.when(r > 2)
            def _():
                for side in SIDES:
                    copies = slot_copies(r + 2, side, False, *ring.far(me, r - 2, side))
                    for c in copies:
                        c.wait_send()
                    start(copies)

    def run_phase(p, _):
        dev, j = ring.piece(p)
        for c in load_piece(False, p, dev, j):
            c.wait()

        @pl.when(p + 1 < phases)
        def _():
            get_ready(p + 1)

        @pl.when(new_part(p) >= 0)
        def _():
            run_new(new_part(p))
        slot = lax.rem(p, 4)
        t0 = (j // 2) * head_tiles
        attend([(t0 + 2 * u, lambda k=k: kslot[slot, k], lambda k=k: vslot[slot, k], None, k == 0, k == nsb - 1)
                for u in range(pairs) for k in range(nsb)])
        return 0

    quad = me // 4
    quads = n // 4

    def new_part(p):
        part = const(-1)
        for s, at in enumerate(new_parts):
            part = jnp.where(p == at, s, part)
        return part

    def part_quad(part):
        near = jnp.where(lax.rem(me // 2, 2) == 0, -1, 1)
        step = jnp.where(part == 1, near, jnp.where(part == 2, -near, part // 3 * 2))
        return lax.rem(quad + step + quads, quads)

    def each_load(part, do):
        m = part_quad(part)
        for d in range(4):
            dev = 4 * m + d

            @pl.when(dev != me)
            def _():
                do(pltpu.make_async_copy(nk_all.at[dev], nkslot.at[dev], nload_sem.at[d, 0]))
                do(pltpu.make_async_copy(nv_all.at[dev], nvslot.at[dev], nload_sem.at[d, 1]))

    def run_new(part):
        m = part_quad(part)
        each_load(part, lambda c: c.wait())
        rowcol = (lax.broadcasted_iota(jnp.int32, (BLK, BLK), 0) - lax.broadcasted_iota(jnp.int32, (BLK, BLK), 1))

        def group(v, _):
            low_tile = jnp.where(part == 0, v == 0, (v == 1) & (m < quad))
            late_keys = jnp.where(part == 0, v == 2, (v == 1) & (m > quad))
            own = jnp.where(low_tile, me, 2 * n - 1 - me)
            block0 = 4 * jnp.where(late_keys, 2 * quads - 1 - m, m)
            blocks = []
            for h in SIDES:
                t0 = h * head_tiles + jnp.where(low_tile, 0, head_tiles // 2)
                for trio in range(pairs // 2):
                    for k in range(4):
                        block = block0 + k
                        at = jnp.where(late_keys, 2 * n - 1 - block, block)
                        i = 2 * h + late_keys.astype(jnp.int32)
                        blocks.append((t0 + 2 * trio, lambda at=at, i=i: nkslot[at, i], lambda at=at, i=i: nvslot[at, i],
                                       rowcol <= (own - block) * BLK, k == 0, k == 3))
            attend(blocks)
            return 0
        lax.fori_loop(0, jnp.where(part == 0, 3, 2), group, 0)

    new_steps = [8 * s + 9 for s in range(hops)] if hops == 4 else [5, 7]
    new_parts = [13, 22, 29, 37] if hops == 4 else [8, 10]
    lax.fori_loop(0, phases, run_phase, 0)

    for c in kept:
        c.wait()
    for idx, num in enumerate(nsends):
        for c in send_new(True, me, 0, num, idx, 0, me):
            c.wait_send()
    def drain(sem):
        for c in send_piece(True, me, 0, sem, 4, me):
            c.wait_send()
    for side in SIDES:
        for slot in range(4):
            drain(way_sem.at[side, slot])
        for slot in SIDES:
            drain(sib_sem.at[side, slot])
    for slot in range(4):
        drain(own_sib_sem.at[slot])


def output_kernel(n, nsb, pairs, scale, x_ref, acc_ref, l_ref, wo_in, q_all, k_in, v_in, k_all, v_all, nk_all, nv_all,
                  y_ref, wo_scr, o_scr, qbuf, kbuf, vbuf, m_scr, l_scr, acc_scr, sem):
    me = lax.axis_index("cp")
    tiles = acc_ref.shape[0]
    head_tiles = tiles // 2
    head_dim = BLK // 2
    weights = pltpu.make_async_copy(wo_in, wo_scr, sem.at[3])
    weights.start()

    def put(t, o_t):
        h, upper, g = t // head_tiles, lax.rem(t, head_tiles) // pairs, lax.rem(t, pairs)
        rows = pl.ds(pl.multiple_of(upper * BLK, BLK), BLK)
        columns = pl.ds(pl.multiple_of((h * pairs + g) * head_dim, head_dim), head_dim)
        o_scr[rows, columns] = o_t.T.astype(BF16)

    def faults_of(t):
        denom = jnp.sum(l_ref[t], axis=0, keepdims=True)
        acc = acc_ref[t]
        fine = (jnp.abs(acc) < jnp.inf) & (denom > 2.0 ** -60) & (denom < 2.0 ** 100)
        faults = jnp.where(fine, 0.0, 1.0).reshape(head_dim // 8, 8, BLK).sum(axis=0)
        return acc * (1.0 / denom), faults

    def some(i, faults):
        for g in range(pairs):
            o_t, more = faults_of(i * pairs + g)
            put(i * pairs + g, o_t)
            faults = faults + more
        return faults
    faults = lax.fori_loop(0, tiles // pairs, some, jnp.zeros((8, BLK), F32))

    @pl.when(jnp.sum(faults) > 0.0)
    def _():
        def tile(t, _):
            @pl.when(jnp.sum(faults_of(t)[1]) > 0.0)
            def _():
                h = t // head_tiles
                upper = lax.rem(t, head_tiles) // pairs
                own = jnp.where(upper == 1, 2 * n - 1 - me, me)
                m_scr[...] = jnp.full(m_scr.shape, NEG, F32)
                l_scr[...] = jnp.zeros_like(l_scr)
                acc_scr[...] = jnp.zeros_like(acc_scr)
                queries = pltpu.make_async_copy(q_all.at[t], qbuf, sem.at[2])
                queries.start()
                queries.wait()

                def fetch(k_src, v_src):
                    copies = (pltpu.make_async_copy(k_src, kbuf, sem.at[0]), pltpu.make_async_copy(v_src, vbuf, sem.at[1]))
                    for c in copies:
                        c.start()
                    for c in copies:
                        c.wait()

                def step(limit):
                    s = dot(kbuf[...], qbuf[...]) * scale
                    rows = lax.broadcasted_iota(jnp.int32, s.shape, 0) - lax.broadcasted_iota(jnp.int32, s.shape, 1)
                    s = jnp.where(rows <= limit, s, -jnp.inf)
                    m_old = m_scr[...]
                    m_new = jnp.maximum(m_old, jnp.max(s, axis=0, keepdims=True))
                    e = jnp.exp(s - m_new)
                    old = jnp.exp(m_old - m_new)
                    m_scr[...] = m_new
                    l_scr[...] = l_scr[...] * old + jnp.sum(e, axis=0, keepdims=True)
                    acc_scr[...] = acc_scr[...] * old + dot(vbuf[...], e.astype(BF16))

                def cached(b, _):
                    dev, rem = b // (2 * nsb), lax.rem(b, 2 * nsb)
                    j, k = 2 * h + rem // nsb, lax.rem(rem, nsb)

                    @pl.when(dev == me)
                    def _():
                        fetch(k_in.at[j, k], v_in.at[j, k])

                    @pl.when(dev != me)
                    def _():
                        fetch(k_all.at[dev, j, k], v_all.at[dev, j, k])
                    step(0 * me + BLK)
                    return 0

                def new(b, _):
                    dev = jnp.where(b < n, b, 2 * n - 1 - b)
                    j = 2 * h + (b >= n).astype(jnp.int32)
                    fetch(nk_all.at[dev, j], nv_all.at[dev, j])
                    step((own - b) * BLK)
                    return 0
                lax.fori_loop(0, 2 * nsb * n, cached, 0)
                lax.fori_loop(0, own + 1, new, 0)
                put(t, acc_scr[...] / l_scr[...])
            return 0
        lax.fori_loop(0, tiles, tile, 0)
    weights.wait()
    width = min(512, wo_scr.shape[1])

    def project(c, _):
        columns = pl.ds(pl.multiple_of(c * width, width), width)
        y_ref[:, columns] = (x_ref[:, columns].astype(F32) + dot(o_scr[...], wo_scr[:, columns])).astype(BF16)
        return 0
    lax.fori_loop(0, wo_scr.shape[1] // width, project, 0)


def solution(mesh):
    n = mesh.shape["cp"]

    def local_step(x_loc, pos_loc, k_loc, v_loc, w_q, w_k, w_v, w_o):
        tok_dev, model_dim = x_loc.shape
        cache_dev, kv_heads, head_dim = k_loc.shape
        q_heads = w_q.shape[1] // head_dim
        group = q_heads // kv_heads
        half = head_dim // 2
        nsb = cache_dev // (2 * BLK)
        pairs = group
        tiles = 2 * q_heads
        inv_freq = jnp.power(jnp.float32(ROPE_BASE), -(jnp.arange(half, dtype=F32) * 2.0 / head_dim))
        angles = pos_loc.astype(F32)[:, None] * inv_freq[None, :]
        cos_a, sin_a = jnp.cos(angles), jnp.sin(angles)
        cos_t = jnp.concatenate([cos_a, cos_a], axis=1)
        sin_t = jnp.concatenate([-sin_a, sin_a], axis=1)

        k_pieces = jnp.transpose(k_loc, (1, 0, 2)).reshape(4, nsb, BLK, head_dim)
        v_pieces = jnp.transpose(v_loc.reshape(2, nsb, BLK, kv_heads, head_dim), (3, 0, 1, 4, 2)).reshape(4, nsb, head_dim, BLK)

        hops = n // 4
        rounds = 4 * (hops - 1) + 2
        phases = 8 + 4 * rounds
        vmem_spec = pl.BlockSpec(memory_space=VMEM)
        dma = pltpu.SemaphoreType.DMA
        scale2 = math.log2(math.e) / math.sqrt(head_dim)
        n_new_sends = 3 + 2 * (hops - 1) + 2 * hops
        hbm_spec = pl.BlockSpec(memory_space=HBM)
        acc, l, q_all, k_all, v_all, nk_all, nv_all = pl.pallas_call(
            functools.partial(attend_kernel, n, nsb, pairs, scale2),
            out_shape=(
                jax.ShapeDtypeStruct((tiles, head_dim, BLK), F32),
                jax.ShapeDtypeStruct((tiles, 8, BLK), F32),
                jax.ShapeDtypeStruct((tiles, head_dim, BLK), BF16),
                jax.ShapeDtypeStruct((n,) + k_pieces.shape, BF16),
                jax.ShapeDtypeStruct((n,) + v_pieces.shape, BF16),
                jax.ShapeDtypeStruct((n, 4, BLK, head_dim), BF16),
                jax.ShapeDtypeStruct((n, 4, head_dim, BLK), BF16),
            ),
            in_specs=[hbm_spec] * 8,
            out_specs=(vmem_spec, vmem_spec) + (hbm_spec,) * 5,
            scratch_shapes=[
                VMEM((tiles, BLK, BLK), BF16),
                VMEM((4, nsb, BLK, head_dim), BF16),
                VMEM((4, nsb, head_dim, BLK), BF16),
                VMEM((n, 4, BLK, head_dim), BF16),
                VMEM((n, 4, head_dim, BLK), BF16),
                VMEM((2, 4, BLK, BLK), BF16),
                VMEM((2, BLK, head_dim), BF16),
                VMEM((16, head_dim), BF16),
                VMEM(x_loc.shape, BF16),
                VMEM(w_q.shape, BF16),
                VMEM((model_dim, 2 * w_k.shape[1]), BF16),
                VMEM((tok_dev, head_dim), F32),
                VMEM((tok_dev, head_dim), F32),
                dma((phases - 4, 2)),
                dma((2, 4, 2)),
                dma((2, 2, 2)),
                dma((4, 2)),
                dma((4 * hops + 1, 2)),
                dma((n_new_sends, 2)),
                dma((4, 2)),
                dma((11,)),
                dma((4, 2)),
            ],
            compiler_params=pltpu.CompilerParams(collective_id=0, has_side_effects=True, vmem_limit_bytes=48 * 2 ** 20),
            name="ring_attention",
        )(x_loc, w_q, w_k, w_v, cos_t, sin_t, k_pieces, v_pieces)

        return pl.pallas_call(
            functools.partial(output_kernel, n, nsb, pairs, 1.0 / math.sqrt(head_dim)),
            out_shape=jax.ShapeDtypeStruct((tok_dev, model_dim), BF16),
            in_specs=[vmem_spec] * 3 + [hbm_spec] * 8,
            out_specs=vmem_spec,
            scratch_shapes=[VMEM(w_o.shape, BF16), VMEM((tok_dev, q_heads * head_dim), BF16), VMEM((head_dim, BLK), BF16),
                            VMEM((BLK, head_dim), BF16), VMEM((head_dim, BLK), BF16), VMEM((1, BLK), F32), VMEM((1, BLK), F32),
                            VMEM((head_dim, BLK), F32), dma((4,))],
            compiler_params=pltpu.CompilerParams(vmem_limit_bytes=40 * 2 ** 20),
            name="output",
        )(x_loc, acc, l, w_o, q_all, k_pieces, v_pieces, k_all, v_all, nk_all, nv_all)

    tok_spec = P(("data", "cp"), None)
    pos_spec = P(("data", "cp"))
    cache_spec = P(("data", "cp"), None, None)
    return jax.shard_map(local_step, mesh=mesh, in_specs=(tok_spec, pos_spec, cache_spec, cache_spec, P(), P(), P(), P()), out_specs=tok_spec, check_vma=False)
```

time: 469 us -> 414 us (0.88)
  Pallas kernels: 429 us -> 401 us
  matrix products: 13.8 us -> 0 us
  local copies, waits for them, and re-layouts: 19.5 us -> 11.1 us
    pallas_call x1, Pallas kernels: 424 us -> 394 us  [local_step(): pl.pallas_call(functools.partial(attend_kernel, n, nsb, pairs, scale2), o...]
    dot_general x4 -> x0, matrix products: 13.8 us -> none  [the longest x1 6.11 us: local_step(): jnp.einsum('kygdt,kgde->yte', o_t, w_out, preferred_element_type=F32)]
    unnamed x34 -> x14, local copies, waits for them, and re-layouts: 9.72 us -> 3.03 us
where the time goes in v2:
time: 414 us
  Pallas kernels  401 us (97%)
  local copies, waits for them, and re-layouts  11.1 us (3%)
    pallas_call x1, Pallas kernels, local_step(): pl.pallas_call(functools.partial(attend_kernel, n, nsb, pairs, scale2), o...  394 us

profile of v2, /device:TPU:22, one launch (start us, length us, event | category | flops | bytes accessed | tf_op | source)
XLA Modules:
  0.0 413.7 jit_solution(7139879775125190130)
XLA Ops:
  0.0 0.0 copy-start.6
  0.0 0.8 convert_element_type.3
  0.8 1.0 fusion
  1.8 0.2 pad_maximum_fusion
  2.1 0.0 copy-done.6
  2.1 1.8 copy.9
  3.8 0.0 copy-start.2
  3.8 0.0 copy-start.4
  3.8 6.3 %copy.10 = bf16[2,8,256,2,128]{2,4,1,0,3:T(8,128)(2,1)} copy(bf16[2,8,256,2,128]{4,3,2,1,0:T(2,128)(2,1)} %bitcast.11) | data formatting | bytes 4194304 | tf_op jit(solution)/shard_map/reshape | solution.py:508
  10.1 0.0 copy-done.2
  10.1 0.0 copy-done.4
  10.1 0.0 copy-start.5
  10.1 1.1 copy-done.5
  11.2 0.0 copy-start
  11.2 0.0 copy-start.1
  11.3 394.1 %ring_attention.1 = (f32[24,128,256]{2,1,0:T(8,128)}, f32[24,8,256]{2,1,0:T(8,128)S(1)}, bf16[24,128,256]{2,1,0:T(8,128)(2,1)S(1)}, bf16[16,4,8,256,128]{4,3,2,1...) custom-call(bf16[512,1536]{1,0:T(8,128)(2,1)S(1)} %copy-done.2, ...), custom_call_target="tpu_custom_call" | custom-call | tf_op jit(solution)/shard_map/ring_attention/pallas_call | solution.py:518
  405.3 0.0 copy-done
  405.3 0.0 copy-done.1
  405.3 0.0 copy-start.3
  405.4 1.9 copy-done.3
  407.2 6.5 %output.1 = bf16[512,1536]{1,0:T(8,128)(2,1)} custom-call(bf16[512,1536]{1,0:T(8,128)(2,1)S(1)} %copy-done.2, f32[24,128,256]{2,1,0:T(8,128)S(1)} %copy-done.3, f32[24,8,256]{2,1,0:T(8,128)S(1)} %get-tuple-element.13.l_ref, bf16[1536,1536]{1,0:T(8,128)(2,1)} %wo_in.1, bf16[24,128,256]{2,1,0:T(8,128)(2,1)S(1)} %get-tuple-element.14.q_all, ...), custom_call_target="tpu_custom_call" | custom-call | tf_op jit(solution)/shard_map/output/pallas_call | solution.py:559
  (1 shorter events, 0.0 us)
Async XLA Ops:
  0.0 2.1 copy-start.6
  3.8 6.3 %copy-start.2 = (bf16[512,1536]{1,0:T(8,128)(2,1)S(1)}, bf16[512,1536]{1,0:T(8,128)(2,1)}, u32[]{:S(2)}) copy-start(bf16[512,1536]{1,0:T(8,128)(2,1)} %x_ref.1) | copy-start | bytes 4718596
  3.8 6.3 %copy-start.4 = (bf16[1536,256]{1,0:T(8,128)(2,1)S(1)}, bf16[1536,256]{1,0:T(8,128)(2,1)}, u32[]{:S(2)}) copy-start(bf16[1536,256]{1,0:T(8,128)(2,1)} %wk_in.1) | copy-start | bytes 2359300
  10.1 1.1 copy-start.5
  11.2 394.1 %copy-start = (bf16[2,4096,128]{2,1,0:T(8,128)(2,1)S(1)}, bf16[2,4096,128]{2,1,0:T(8,128)(2,1)}, u32[]{:S(2)}) copy-start(bf16[2,4096,128]{2,1,0:T(8,128)(2,1)} %copy.9) | copy-start | bytes 6291460
  11.2 394.1 %copy-start.1 = (bf16[2,8,256,2,128]{2,4,1,0,3:T(8,128)(2,1)S(1)}, bf16[2,8,256,2,128]{2,4,1,0,3:T(8,128)(2,1)}, u32[]{:S(2)}) copy-start(bf16[2,8,256,2,128]{2,4,1,0,3:T(8,128)(2,1)} %copy.10) | copy-start | bytes 6291460
  405.3 1.9 copy-start.3

commit v3 on v2

--- a/solution.py
+++ b/solution.py
@@ -49,9 +49,9 @@
     return jnp.dot(a, b, preferred_element_type=F32)
 
 
-def attend_kernel(n, nsb, pairs, scale2, x_in, wq_in, wk_in, wv_in, cos_in, sin_in, k_in, v_in,
+def attend_kernel(n, nsb, pairs, scale2, x_ref, wq_in, wk_ref, wv_ref, cos_ref, sin_ref, k_in, vn_ref,
                   acc_out, l_out, q_all, k_all, v_all, nk_all, nv_all,
-                  q_scr, kslot, vslot, nkslot, nvslot, p_scr, kfirst, ones_scr, x_scr, wq_scr, wkv_scr, cos_scr, sin_scr,
+                  q_scr, kslot, vslot, nkslot, nvslot, p_scr, kfirst, ones_scr, wq_scr, vt_scr,
                   recv_sem, way_sem, sib_sem, own_sib_sem, nrecv_sem, nsend_sem, load_sem, misc_sem, nload_sem):
     ring = Ring(n)
     me, sib, right, left, hops = ring.me, ring.sib, ring.right, ring.left, ring.hops
@@ -68,7 +68,7 @@
 
     def send_piece(from_own, dev, j, pair_sem, phase, to):
         ksrc = k_in.at[j] if from_own else k_all.at[dev, j]
-        vsrc = v_in.at[j] if from_own else v_all.at[dev, j]
+        vsrc = v_all.at[dev, j]
         return (send(ksrc, k_all.at[dev, j], pair_sem.at[0], recv_sem.at[phase - 4, 0], to),
                 send(vsrc, v_all.at[dev, j], pair_sem.at[1], recv_sem.at[phase - 4, 1], to))
 
@@ -118,6 +118,10 @@
             start(copies)
             nsends.append(num)
 
+    then = [pltpu.make_async_copy(wq_in, wq_scr, misc_sem.at[0])]
+    then += [pltpu.make_async_copy(k_in.at[2 * h, 0], kfirst.at[h], misc_sem.at[1 + h]) for h in SIDES]
+    start(then)
+
     barrier = pltpu.get_barrier_semaphore()
     for other in (left, right, sib):
         pl.semaphore_signal(barrier, inc=1, device_id={"cp": other}, device_id_type=MESH_ID)
@@ -130,28 +134,16 @@
     def slot_copies(slot, side, own, dev, j):
         return send_piece(own, dev, j, way_sem.at[side, lax.rem(slot, 4)], 4 + 4 * slot + side, (right, left)[side])
 
-    own_slot(const(1))
-    for j in range(4):
-        start(send_piece(True, me, j, own_sib_sem.at[j], 4 + j, sib))
+    first_round = [slot_copies(const(1), side, True, me, 2 * side) for side in SIDES]
+    first_round += [send_piece(True, me, j, own_sib_sem.at[j], 4 + j, sib) for j in range(4)]
+    start([c[0] for c in first_round])
 
     def load_piece(own, p, dev, j):
         ksrc = k_in.at[j] if own else k_all.at[dev, j]
-        vsrc = v_in.at[j] if own else v_all.at[dev, j]
+        vsrc = v_all.at[dev, j]
         slot = lax.rem(p, 4)
         return (pltpu.make_async_copy(ksrc, kslot.at[slot], load_sem.at[slot, 0]),
                 pltpu.make_async_copy(vsrc, vslot.at[slot], load_sem.at[slot, 1]))
-
-    kv_width = wk_in.shape[1]
-    first = [pltpu.make_async_copy(x_in, x_scr, misc_sem.at[0]),
-             pltpu.make_async_copy(wk_in, wkv_scr.at[:, pl.ds(0, kv_width)], misc_sem.at[1]),
-             pltpu.make_async_copy(wv_in, wkv_scr.at[:, pl.ds(kv_width, kv_width)], misc_sem.at[2]),
-             pltpu.make_async_copy(cos_in, cos_scr, misc_sem.at[3]),
-             pltpu.make_async_copy(sin_in, sin_scr, misc_sem.at[4])]
-    then = [pltpu.make_async_copy(wq_in, wq_scr, misc_sem.at[5])]
-    then += [pltpu.make_async_copy(k_in.at[2 * h, 0], kfirst.at[h], misc_sem.at[6 + h]) for h in SIDES]
-    start(first)
-    start(then)
-    start(load_piece(True, const(0), me, 0))
 
     ones_scr[...] = jnp.where(lax.broadcasted_iota(jnp.int32, ones_scr.shape, 1) == 0, 1.0, 0.0).astype(BF16)
 
@@ -161,29 +153,38 @@
         l_out[t] = jnp.zeros(l_out.shape[1:], F32)
         return 0
     lax.fori_loop(0, tiles, clear, 0)
-    for c in first:
-        c.wait()
+
+    def transpose(j, _):
+        for k in range(nsb):
+            vt_scr[j, k] = vn_ref[j, k].T
+        return 0
+    lax.fori_loop(0, 4, transpose, 0)
+    own_values = pltpu.make_async_copy(vt_scr, v_all.at[me], misc_sem.at[3])
+    own_values.start()
 
     head_dim = BLK // 2
 
     def turned(u):
         u = u.astype(BF16).astype(F32)
-        return (u * cos_scr[...] + pltpu.roll(u, head_dim // 2, 1) * sin_scr[...]).astype(BF16)
-
-    new_kv = dot(x_scr[...], wkv_scr[...])
+        return (u * cos_ref[...] + pltpu.roll(u, head_dim // 2, 1) * sin_ref[...]).astype(BF16)
+
+    new_k, new_v = dot(x_ref[...], wk_ref[...]), dot(x_ref[...], wv_ref[...])
     for h in SIDES:
-        keys = turned(new_kv[:, h * head_dim:(h + 1) * head_dim])
-        values = new_kv[:, kv_width + h * head_dim:kv_width + (h + 1) * head_dim].T.astype(BF16)
+        keys = turned(new_k[:, h * head_dim:(h + 1) * head_dim])
+        values = new_v[:, h * head_dim:(h + 1) * head_dim].T.astype(BF16)
         for half in SIDES:
             nkslot[me, 2 * h + half] = keys[half * BLK:(half + 1) * BLK]
             nvslot[me, 2 * h + half] = values[:, half * BLK:(half + 1) * BLK]
+    own_values.wait()
+    start([c[1] for c in first_round])
+    start(load_piece(True, const(0), me, 0))
     for c in then:
         c.wait()
     heads = 4
 
     def project(c, _):
         width = heads * head_dim
-        z = dot(x_scr[...], wq_scr[:, pl.ds(pl.multiple_of(c * width, width), width)])
+        z = dot(x_ref[...], wq_scr[:, pl.ds(pl.multiple_of(c * width, width), width)])
         for i in range(heads):
             head = c * heads + i
             t = (head // pairs) * head_tiles + lax.rem(head, pairs)
@@ -198,9 +199,9 @@
         nsends.append(4)
     own_slot(const(2))
     own_slot(const(3))
-    kept = [pltpu.make_async_copy(q_scr.at[:, pl.ds(0, head_dim)], q_all, misc_sem.at[8]),
-            pltpu.make_async_copy(nkslot.at[me], nk_all.at[me], misc_sem.at[9]),
-            pltpu.make_async_copy(nvslot.at[me], nv_all.at[me], misc_sem.at[10])]
+    kept = [pltpu.make_async_copy(q_scr.at[:, pl.ds(0, head_dim)], q_all, misc_sem.at[4]),
+            pltpu.make_async_copy(nkslot.at[me], nk_all.at[me], misc_sem.at[5]),
+            pltpu.make_async_copy(nvslot.at[me], nv_all.at[me], misc_sem.at[6])]
     start(kept)
 
     def lhs_keys(keys):
@@ -302,12 +303,14 @@
 
     def run_phase(p, _):
         dev, j = ring.piece(p)
+
+        def ready(q, _):
+            get_ready(q)
+            return 0
+        last = phases - 4
+        lax.fori_loop(jnp.where(p == last, p, p + 1), jnp.where(p == last - 1, p + 1, jnp.minimum(p + 2, phases)), ready, 0)
         for c in load_piece(False, p, dev, j):
             c.wait()
-
-        @pl.when(p + 1 < phases)
-        def _():
-            get_ready(p + 1)
 
         @pl.when(new_part(p) >= 0)
         def _():
@@ -334,22 +337,25 @@
 
     def each_load(part, do):
         m = part_quad(part)
-        for d in range(4):
+
+        def load(d, _):
             dev = 4 * m + d
 
             @pl.when(dev != me)
             def _():
                 do(pltpu.make_async_copy(nk_all.at[dev], nkslot.at[dev], nload_sem.at[d, 0]))
                 do(pltpu.make_async_copy(nv_all.at[dev], nvslot.at[dev], nload_sem.at[d, 1]))
+            return 0
+        lax.fori_loop(0, 4, load, 0)
 
     def run_new(part):
         m = part_quad(part)
         each_load(part, lambda c: c.wait())
         rowcol = (lax.broadcasted_iota(jnp.int32, (BLK, BLK), 0) - lax.broadcasted_iota(jnp.int32, (BLK, BLK), 1))
 
-        def group(v, _):
-            low_tile = jnp.where(part == 0, v == 0, (v == 1) & (m < quad))
-            late_keys = jnp.where(part == 0, v == 2, (v == 1) & (m > quad))
+        def group(v, masked):
+            low_tile = (v == 0) & masked | (part > 0) & (v == 1) & (m < quad)
+            late_keys = (v == 2) | (part > 0) & (v == 1) & (m > quad)
             own = jnp.where(low_tile, me, 2 * n - 1 - me)
             block0 = 4 * jnp.where(late_keys, 2 * quads - 1 - m, m)
             blocks = []
@@ -361,10 +367,14 @@
                         at = jnp.where(late_keys, 2 * n - 1 - block, block)
                         i = 2 * h + late_keys.astype(jnp.int32)
                         blocks.append((t0 + 2 * trio, lambda at=at, i=i: nkslot[at, i], lambda at=at, i=i: nvslot[at, i],
-                                       rowcol <= (own - block) * BLK, k == 0, k == 3))
+                                       rowcol <= (own - block) * BLK if masked else None, k == 0, k == 3))
             attend(blocks)
             return 0
-        lax.fori_loop(0, jnp.where(part == 0, 3, 2), group, 0)
+
+        @pl.when(part == 0)
+        def _():
+            lax.fori_loop(0, 2, lambda v, _: group(2 * v, True), 0)
+        lax.fori_loop(jnp.where(part == 0, 1, 0), 2, lambda v, _: group(v, False), 0)
 
     new_steps = [8 * s + 9 for s in range(hops)] if hops == 4 else [5, 7]
     new_parts = [13, 22, 29, 37] if hops == 4 else [8, 10]
@@ -387,14 +397,12 @@
         drain(own_sib_sem.at[slot])
 
 
-def output_kernel(n, nsb, pairs, scale, x_ref, acc_ref, l_ref, wo_in, q_all, k_in, v_in, k_all, v_all, nk_all, nv_all,
-                  y_ref, wo_scr, o_scr, qbuf, kbuf, vbuf, m_scr, l_scr, acc_scr, sem):
+def output_kernel(n, nsb, pairs, scale, x_ref, acc_ref, l_ref, wo_ref, q_all, k_in, k_all, v_all, nk_all, nv_all,
+                  y_ref, o_scr, qbuf, kbuf, vbuf, m_scr, l_scr, acc_scr, sem):
     me = lax.axis_index("cp")
     tiles = acc_ref.shape[0]
     head_tiles = tiles // 2
     head_dim = BLK // 2
-    weights = pltpu.make_async_copy(wo_in, wo_scr, sem.at[3])
-    weights.start()
 
     def put(t, o_t):
         h, upper, g = t // head_tiles, lax.rem(t, head_tiles) // pairs, lax.rem(t, pairs)
@@ -457,7 +465,7 @@
 
                     @pl.when(dev == me)
                     def _():
-                        fetch(k_in.at[j, k], v_in.at[j, k])
+                        fetch(k_in.at[j, k], v_all.at[dev, j, k])
 
                     @pl.when(dev != me)
                     def _():
@@ -476,14 +484,17 @@
                 put(t, acc_scr[...] / l_scr[...])
             return 0
         lax.fori_loop(0, tiles, tile, 0)
-    weights.wait()
-    width = min(512, wo_scr.shape[1])
+    width = min(512, wo_ref.shape[1])
 
     def project(c, _):
         columns = pl.ds(pl.multiple_of(c * width, width), width)
-        y_ref[:, columns] = (x_ref[:, columns].astype(F32) + dot(o_scr[...], wo_scr[:, columns])).astype(BF16)
+        y_ref[:, columns] = (x_ref[:, columns].astype(F32) + dot(o_scr[...], wo_ref[:, columns])).astype(BF16)
         return 0
-    lax.fori_loop(0, wo_scr.shape[1] // width, project, 0)
+    lax.fori_loop(0, wo_ref.shape[1] // width, project, 0)
+
+
+def in_hbm(a):
+    return pltpu.with_memory_space_constraint(a, HBM)
 
 
 def solution(mesh):
@@ -505,7 +516,7 @@
         sin_t = jnp.concatenate([-sin_a, sin_a], axis=1)
 
         k_pieces = jnp.transpose(k_loc, (1, 0, 2)).reshape(4, nsb, BLK, head_dim)
-        v_pieces = jnp.transpose(v_loc.reshape(2, nsb, BLK, kv_heads, head_dim), (3, 0, 1, 4, 2)).reshape(4, nsb, head_dim, BLK)
+        v_pieces = jnp.transpose(v_loc, (1, 0, 2)).reshape(4, nsb, BLK, head_dim)
 
         hops = n // 4
         rounds = 4 * (hops - 1) + 2
@@ -520,13 +531,13 @@
             out_shape=(
                 jax.ShapeDtypeStruct((tiles, head_dim, BLK), F32),
                 jax.ShapeDtypeStruct((tiles, 8, BLK), F32),
-                jax.ShapeDtypeStruct((tiles, head_dim, BLK), BF16),
-                jax.ShapeDtypeStruct((n,) + k_pieces.shape, BF16),
-                jax.ShapeDtypeStruct((n,) + v_pieces.shape, BF16),
-                jax.ShapeDtypeStruct((n, 4, BLK, head_dim), BF16),
-                jax.ShapeDtypeStruct((n, 4, head_dim, BLK), BF16),
+                HBM((tiles, head_dim, BLK), BF16),
+                HBM((n,) + k_pieces.shape, BF16),
+                HBM((n, 4, nsb, head_dim, BLK), BF16),
+                HBM((n, 4, BLK, head_dim), BF16),
+                HBM((n, 4, head_dim, BLK), BF16),
             ),
-            in_specs=[hbm_spec] * 8,
+            in_specs=[vmem_spec, hbm_spec] + [vmem_spec] * 4 + [hbm_spec, vmem_spec],
             out_specs=(vmem_spec, vmem_spec) + (hbm_spec,) * 5,
             scratch_shapes=[
                 VMEM((tiles, BLK, BLK), BF16),
@@ -537,11 +548,8 @@
                 VMEM((2, 4, BLK, BLK), BF16),
                 VMEM((2, BLK, head_dim), BF16),
                 VMEM((16, head_dim), BF16),
-                VMEM(x_loc.shape, BF16),
                 VMEM(w_q.shape, BF16),
-                VMEM((model_dim, 2 * w_k.shape[1]), BF16),
-                VMEM((tok_dev, head_dim), F32),
-                VMEM((tok_dev, head_dim), F32),
+                VMEM((4, nsb, head_dim, BLK), BF16),
                 dma((phases - 4, 2)),
                 dma((2, 4, 2)),
                 dma((2, 2, 2)),
@@ -549,24 +557,24 @@
                 dma((4 * hops + 1, 2)),
                 dma((n_new_sends, 2)),
                 dma((4, 2)),
-                dma((11,)),
+                dma((7,)),
                 dma((4, 2)),
             ],
-            compiler_params=pltpu.CompilerParams(collective_id=0, has_side_effects=True, vmem_limit_bytes=48 * 2 ** 20),
+            compiler_params=pltpu.CompilerParams(collective_id=0, has_side_effects=True, vmem_limit_bytes=36 * 2 ** 20),
             name="ring_attention",
-        )(x_loc, w_q, w_k, w_v, cos_t, sin_t, k_pieces, v_pieces)
+        )(x_loc, in_hbm(w_q), w_k, w_v, cos_t, sin_t, in_hbm(k_pieces), v_pieces)
 
         return pl.pallas_call(
             functools.partial(output_kernel, n, nsb, pairs, 1.0 / math.sqrt(head_dim)),
             out_shape=jax.ShapeDtypeStruct((tok_dev, model_dim), BF16),
-            in_specs=[vmem_spec] * 3 + [hbm_spec] * 8,
+            in_specs=[vmem_spec] * 4 + [hbm_spec] * 6,
             out_specs=vmem_spec,
-            scratch_shapes=[VMEM(w_o.shape, BF16), VMEM((tok_dev, q_heads * head_dim), BF16), VMEM((head_dim, BLK), BF16),
+            scratch_shapes=[VMEM((tok_dev, q_heads * head_dim), BF16), VMEM((head_dim, BLK), BF16),
                             VMEM((BLK, head_dim), BF16), VMEM((head_dim, BLK), BF16), VMEM((1, BLK), F32), VMEM((1, BLK), F32),
-                            VMEM((head_dim, BLK), F32), dma((4,))],
-            compiler_params=pltpu.CompilerParams(vmem_limit_bytes=40 * 2 ** 20),
+                            VMEM((head_dim, BLK), F32), dma((3,))],
+            compiler_params=pltpu.CompilerParams(vmem_limit_bytes=16 * 2 ** 20),
             name="output",
-        )(x_loc, acc, l, w_o, q_all, k_pieces, v_pieces, k_all, v_all, nk_all, nv_all)
+        )(x_loc, acc, l, w_o, *(in_hbm(a) for a in (q_all, k_pieces, k_all, v_all, nk_all, nv_all)))
 
     tok_spec = P(("data", "cp"), None)
     pos_spec = P(("data", "cp"))

time: 414 us -> 403 us (0.973)
  local copies, waits for them, and re-layouts: 11.1 us -> 3.43 us
    reshape x1 -> x0, local copies, waits for them, and re-layouts: 6.27 us -> none  [local_step(): v_loc.reshape(2, nsb, BLK, kv_heads, head_dim)]
where the time goes in v3:
time: 403 us; the launch traced here: 402 us
  Pallas kernels  397 us (99%)
    pallas_call x1, Pallas kernels, local_step(): pl.pallas_call(functools.partial(attend_kernel, n, nsb, pairs, scale2), o...  391 us

profile of v3, /device:TPU:22, one launch (start us, length us, event | category | flops | bytes accessed | tf_op | source)
XLA Modules:
  0.0 402.5 jit_solution(16660947036546805368)
XLA Ops:
  0.0 0.0 copy-start.3
  0.0 0.8 convert_element_type.3
  0.8 0.0 copy-start.4
  0.9 1.0 fusion
  1.8 0.2 pad_maximum_fusion
  2.1 0.0 copy-done.3
  2.1 1.6 copy.9
  3.7 0.0 copy-start
  3.7 0.0 copy-start.1
  3.7 0.0 copy-start.2
  3.7 0.0 copy-done.4
  3.7 0.3 copy.10
  4.0 0.0 slice-start
  4.0 1.1 copy-done
  5.1 0.2 copy-done.1
  5.3 0.2 copy-done.2
  5.5 0.0 slice-start.1
  5.5 391.4 %ring_attention.1 = (f32[24,128,256]{2,1,0:T(8,128)S(1)}, f32[24,8,256]{2,1,0:T(8,128)S(1)}, bf16[24,128,256]{2,1,0:T(8,128)(2,1)}, bf16[16,4,8,256,128]{4,3,2,1...) custom-call(bf16[512,1536]{1,0:T(8,128)(2,1)S(1)} %copy-done, ...), custom_call_target="tpu_custom_call" | custom-call | tf_op jit(solution)/shard_map/ring_attention/pallas_call | solution.py:529
  397.0 0.0 slice-done
  397.0 0.0 slice-done.1
  397.0 5.3 %output.1 = bf16[512,1536]{1,0:T(8,128)(2,1)} custom-call(bf16[512,1536]{1,0:T(8,128)(2,1)S(1)} %copy-done, f32[24,128,256]{2,1,0:T(8,128)S(1)} %get-tuple-element.12.acc_ref, f32[24,8,256]{2,1,0:T(8,128)S(1)} %get-tuple-element.13.l_ref, bf16[1536,1536]{1,0:T(8,128)(2,1)S(1)} %bitcast.6, bf16[24,128,256]{2,1,0:T(8,128)(2,1)} %get-tuple-element.14.q_all, ...), custom_call_target="tpu_custom_call" | custom-call | tf_op jit(solution)/shard_map/output/pallas_call | solution.py:567
  (2 shorter events, 0.0 us)
Async XLA Ops:
  0.0 2.1 copy-start.3
  0.8 2.8 copy-start.4
  3.7 1.4 copy-start
  3.7 1.6 copy-start.1
  3.7 1.8 copy-start.2
  4.0 393.0 %slice-start = ((s8[4718592]{0:T(1024)(128)(4,1)}), s8[4194304]{0:T(1024)(128)(4,1)S(1)}, s32[]{:S(2)}) async-start(s8[4718592]{0:T(1024)(128)(4,1)} %bitcast.5), calls=%async_computation | async-start | bytes 8388608
  5.5 391.5 %slice-start.1 = ((s8[4718592]{0:T(1024)(128)(4,1)}), s8[524288]{0:T(1024)(128)(4,1)S(1)}, s32[]{:S(2)}) async-start(s8[4718592]{0:T(1024)(128)(4,1)} %bitcast.5), calls=%async_computation.1 | async-start | bytes 1048576

commit v4 on v3

--- a/solution.py
+++ b/solution.py
@@ -30,9 +30,18 @@
         self.hops = n // 4
         self.rounds = 4 * (self.hops - 1) + 2
         self.phases = 8 + 4 * self.rounds
+        self.direct = self.rounds - 3
 
     def round_of(self, p):
         return (p - 8) // 4 + 1, lax.rem(p - 8, 4)
+
+    def slot(self, p):
+        r, i = self.round_of(jnp.maximum(p, 8))
+        return jnp.where(self.arrives_direct(p), 4 + 2 * (r - self.direct) + i, lax.rem(p, 4))
+
+    def arrives_direct(self, p):
+        r, i = self.round_of(jnp.maximum(p, 8))
+        return (i < 2) & (r >= self.direct) & (p >= 8)
 
     def far(self, base, r, side):
         s = (r - 1) // 4 + 1
@@ -49,13 +58,13 @@
     return jnp.dot(a, b, preferred_element_type=F32)
 
 
-def attend_kernel(n, nsb, pairs, scale2, x_ref, wq_in, wk_ref, wv_ref, cos_ref, sin_ref, k_in, vn_ref,
+def attend_kernel(n, nsb, pairs, scale2, x_in, wq_in, wk_in, wv_in, cos_ref, sin_ref, k_in, vn_ref,
                   acc_out, l_out, q_all, k_all, v_all, nk_all, nv_all,
-                  q_scr, kslot, vslot, nkslot, nvslot, p_scr, kfirst, ones_scr, wq_scr, vt_scr,
-                  recv_sem, way_sem, sib_sem, own_sib_sem, nrecv_sem, nsend_sem, load_sem, misc_sem, nload_sem):
+                  q_scr, kslot, vslot, nkslot, nvslot, p_scr, kfirst, ones_scr, x_ref, wk_ref, wv_ref, wq_scr, vt_scr,
+                  recv_sem, way_sem, sib_sem, own_sib_sem, nrecv_sem, nsend_sem, load_sem, keep_sem, misc_sem, nload_sem):
     ring = Ring(n)
     me, sib, right, left, hops = ring.me, ring.sib, ring.right, ring.left, ring.hops
-    rounds, phases = ring.rounds, ring.phases
+    rounds, phases, direct = ring.rounds, ring.phases, ring.direct
     tiles = q_scr.shape[0]
     head_tiles = tiles // 2
 
@@ -66,11 +75,15 @@
         return pltpu.make_async_remote_copy(src_ref=src, dst_ref=dst, send_sem=send_sem, recv_sem=recv,
                                             device_id={"cp": to}, device_id_type=MESH_ID)
 
-    def send_piece(from_own, dev, j, pair_sem, phase, to):
-        ksrc = k_in.at[j] if from_own else k_all.at[dev, j]
-        vsrc = v_all.at[dev, j]
-        return (send(ksrc, k_all.at[dev, j], pair_sem.at[0], recv_sem.at[phase - 4, 0], to),
-                send(vsrc, v_all.at[dev, j], pair_sem.at[1], recv_sem.at[phase - 4, 1], to))
+    def send_piece(from_own, dev, j, pair_sem, phase, to, src_slot=None, dst_slot=None):
+        kdst, vdst = k_all.at[dev, j], v_all.at[dev, j]
+        ksrc, vsrc = (k_in.at[j] if from_own else kdst), vdst
+        if src_slot is not None:
+            ksrc, vsrc = kslot.at[src_slot], vslot.at[src_slot]
+        if dst_slot is not None:
+            kdst, vdst = kslot.at[dst_slot], vslot.at[dst_slot]
+        return (send(ksrc, kdst, pair_sem.at[0], recv_sem.at[phase - 4, 0], to),
+                send(vsrc, vdst, pair_sem.at[1], recv_sem.at[phase - 4, 1], to))
 
     def send_new(from_own, dev, lo, num, idx, ridx, to):
         ksrc = (nkslot if from_own else nk_all).at[dev, pl.ds(lo, num)]
@@ -120,6 +133,9 @@
 
     then = [pltpu.make_async_copy(wq_in, wq_scr, misc_sem.at[0])]
     then += [pltpu.make_async_copy(k_in.at[2 * h, 0], kfirst.at[h], misc_sem.at[1 + h]) for h in SIDES]
+    first = [pltpu.make_async_copy(a, b, misc_sem.at[7 + i])
+             for i, (a, b) in enumerate(((x_in, x_ref), (wk_in, wk_ref), (wv_in, wv_ref)))]
+    start(first)
     start(then)
 
     barrier = pltpu.get_barrier_semaphore()
@@ -129,10 +145,12 @@
 
     def own_slot(slot):
         for side in SIDES:
-            start(slot_copies(slot, side, True, me, lax.rem(slot - 1 + 2 * side, 4)))
-
-    def slot_copies(slot, side, own, dev, j):
-        return send_piece(own, dev, j, way_sem.at[side, lax.rem(slot, 4)], 4 + 4 * slot + side, (right, left)[side])
+            start(slot_copies(const(slot), side, True, me, (slot - 1 + 2 * side) % 4, slot >= direct))
+
+    def slot_copies(slot, side, own, dev, j, to_vmem=False):
+        phase = 4 + 4 * slot + side
+        return send_piece(own, dev, j, way_sem.at[side, lax.rem(slot, 4)], phase, (right, left)[side],
+                          dst_slot=ring.slot(phase) if to_vmem else None)
 
     first_round = [slot_copies(const(1), side, True, me, 2 * side) for side in SIDES]
     first_round += [send_piece(True, me, j, own_sib_sem.at[j], 4 + j, sib) for j in range(4)]
@@ -144,6 +162,10 @@
         slot = lax.rem(p, 4)
         return (pltpu.make_async_copy(ksrc, kslot.at[slot], load_sem.at[slot, 0]),
                 pltpu.make_async_copy(vsrc, vslot.at[slot], load_sem.at[slot, 1]))
+
+    def keep_piece(slot, dev, j):
+        return (pltpu.make_async_copy(kslot.at[slot], k_all.at[dev, j], keep_sem.at[slot - 4, 0]),
+                pltpu.make_async_copy(vslot.at[slot], v_all.at[dev, j], keep_sem.at[slot - 4, 1]))
 
     ones_scr[...] = jnp.where(lax.broadcasted_iota(jnp.int32, ones_scr.shape, 1) == 0, 1.0, 0.0).astype(BF16)
 
@@ -161,6 +183,8 @@
     lax.fori_loop(0, 4, transpose, 0)
     own_values = pltpu.make_async_copy(vt_scr, v_all.at[me], misc_sem.at[3])
     own_values.start()
+    for c in first:
+        c.wait()
 
     head_dim = BLK // 2
 
@@ -197,8 +221,8 @@
     for other, ridx in ((right, 0), (left, 1), (sib, 4 * hops)):
         start(send_new(True, me, 0, 4, len(nsends), ridx, other))
         nsends.append(4)
-    own_slot(const(2))
-    own_slot(const(3))
+    own_slot(2)
+    own_slot(3)
     kept = [pltpu.make_async_copy(q_scr.at[:, pl.ds(0, head_dim)], q_all, misc_sem.at[4]),
             pltpu.make_async_copy(nkslot.at[me], nk_all.at[me], misc_sem.at[5]),
             pltpu.make_async_copy(nvslot.at[me], nv_all.at[me], misc_sem.at[6])]
@@ -249,6 +273,7 @@
 
     def get_ready(p):
         dev, j = ring.piece(p)
+        arrived = ring.arrives_direct(p)
 
         @pl.when(p < 4)
         def _():
@@ -257,7 +282,14 @@
         @pl.when(p >= 4)
         def _():
             recv_wait(p, dev, j)
+
+        @pl.when((p >= 4) & ~arrived)
+        def _():
             start(load_piece(False, p, dev, j))
+
+        @pl.when(arrived)
+        def _():
+            start(keep_piece(ring.slot(p), dev, j))
 
         for s, at in enumerate(new_steps):
             @pl.when(p == at)
@@ -279,27 +311,35 @@
 
         @pl.when((p >= 8) & (i < 2))
         def _():
-            copies = send_piece(False, dev, j, sib_sem.at[i, lax.rem(r, 2)], p + 2, sib)
+            sem = sib_sem.at[i, lax.rem(r, 2)]
 
             @pl.when(r > 2)
             def _():
-                for c in copies:
+                for c in send_piece(False, dev, j, sem, p + 2, sib):
                     c.wait_send()
-            start(copies)
+
+            @pl.when(~arrived)
+            def _():
+                start(send_piece(False, dev, j, sem, p + 2, sib))
+
+            @pl.when(arrived)
+            def _():
+                start(send_piece(False, dev, j, sem, p + 2, sib, src_slot=ring.slot(p)))
 
         @pl.when((p >= 8) & (i == 0) & (r > 1) & (r + 2 <= rounds))
         def _():
             @pl.when(r == 2)
             def _():
-                own_slot(r + 2)
-
-            @pl.when(r > 2)
-            def _():
-                for side in SIDES:
-                    copies = slot_copies(r + 2, side, False, *ring.far(me, r - 2, side))
-                    for c in copies:
-                        c.wait_send()
-                    start(copies)
+                own_slot(4)
+
+            for to_vmem in (False, True):
+                @pl.when((r > 2) & ((r + 2 >= direct) == to_vmem))
+                def _():
+                    for side in SIDES:
+                        copies = slot_copies(r + 2, side, False, *ring.far(me, r - 2, side), to_vmem)
+                        for c in copies:
+                            c.wait_send()
+                        start(copies)
 
     def run_phase(p, _):
         dev, j = ring.piece(p)
@@ -307,15 +347,18 @@
         def ready(q, _):
             get_ready(q)
             return 0
-        last = phases - 4
-        lax.fori_loop(jnp.where(p == last, p, p + 1), jnp.where(p == last - 1, p + 1, jnp.minimum(p + 2, phases)), ready, 0)
-        for c in load_piece(False, p, dev, j):
-            c.wait()
+        late, late_next = ((lax.rem(q, 4) == 0) & ring.arrives_direct(q) for q in (p, p + 1))
+        lax.fori_loop(jnp.where(late, p, p + 1), jnp.where(late_next, p + 1, jnp.minimum(p + 2, phases)), ready, 0)
+
+        @pl.when(~ring.arrives_direct(p))
+        def _():
+            for c in load_piece(False, p, dev, j):
+                c.wait()
 
         @pl.when(new_part(p) >= 0)
         def _():
             run_new(new_part(p))
-        slot = lax.rem(p, 4)
+        slot = ring.slot(p)
         t0 = (j // 2) * head_tiles
         attend([(t0 + 2 * u, lambda k=k: kslot[slot, k], lambda k=k: vslot[slot, k], None, k == 0, k == nsb - 1)
                 for u in range(pairs) for k in range(nsb)])
@@ -382,6 +425,9 @@
 
     for c in kept:
         c.wait()
+    for slot in range(4, kslot.shape[0]):
+        for c in keep_piece(slot, me, 0):
+            c.wait()
     for idx, num in enumerate(nsends):
         for c in send_new(True, me, 0, num, idx, 0, me):
             c.wait_send()
@@ -537,17 +583,20 @@
                 HBM((n, 4, BLK, head_dim), BF16),
                 HBM((n, 4, head_dim, BLK), BF16),
             ),
-            in_specs=[vmem_spec, hbm_spec] + [vmem_spec] * 4 + [hbm_spec, vmem_spec],
+            in_specs=[hbm_spec] * 4 + [vmem_spec] * 2 + [hbm_spec, vmem_spec],
             out_specs=(vmem_spec, vmem_spec) + (hbm_spec,) * 5,
             scratch_shapes=[
                 VMEM((tiles, BLK, BLK), BF16),
-                VMEM((4, nsb, BLK, head_dim), BF16),
-                VMEM((4, nsb, head_dim, BLK), BF16),
+                VMEM((12, nsb, BLK, head_dim), BF16),
+                VMEM((12, nsb, head_dim, BLK), BF16),
                 VMEM((n, 4, BLK, head_dim), BF16),
                 VMEM((n, 4, head_dim, BLK), BF16),
                 VMEM((2, 4, BLK, BLK), BF16),
                 VMEM((2, BLK, head_dim), BF16),
                 VMEM((16, head_dim), BF16),
+                VMEM(x_loc.shape, BF16),
+                VMEM(w_k.shape, BF16),
+                VMEM(w_v.shape, BF16),
                 VMEM(w_q.shape, BF16),
                 VMEM((4, nsb, head_dim, BLK), BF16),
                 dma((phases - 4, 2)),
@@ -557,12 +606,13 @@
                 dma((4 * hops + 1, 2)),
                 dma((n_new_sends, 2)),
                 dma((4, 2)),
-                dma((7,)),
+                dma((8, 2)),
+                dma((10,)),
                 dma((4, 2)),
             ],
-            compiler_params=pltpu.CompilerParams(collective_id=0, has_side_effects=True, vmem_limit_bytes=36 * 2 ** 20),
+            compiler_params=pltpu.CompilerParams(collective_id=0, has_side_effects=True, vmem_limit_bytes=44 * 2 ** 20),
             name="ring_attention",
-        )(x_loc, in_hbm(w_q), w_k, w_v, cos_t, sin_t, in_hbm(k_pieces), v_pieces)
+        )(in_hbm(x_loc), in_hbm(w_q), in_hbm(w_k), in_hbm(w_v), cos_t, sin_t, in_hbm(k_pieces), v_pieces)
 
         return pl.pallas_call(
             functools.partial(output_kernel, n, nsb, pairs, 1.0 / math.sqrt(head_dim)),

time: 403 us -> 400 us (level)
  no operation moved by 1% of the time
where the time goes in v4:
time: 400 us
  Pallas kernels  396 us (99%)
    pallas_call x1, Pallas kernels, local_step(): pl.pallas_call(functools.partial(attend_kernel, n, nsb, pairs, scale2), o...  391 us

profile of v4, /device:TPU:22, one launch (start us, length us, event | category | flops | bytes accessed | tf_op | source)
XLA Modules:
  0.0 400.3 jit_solution(6338588905169604591)
XLA Ops:
  0.0 0.0 copy-start.1
  0.0 0.8 convert_element_type.3
  0.8 0.0 copy-start.2
  0.9 1.0 fusion
  1.8 0.2 pad_maximum_fusion
  2.1 0.0 copy-done.1
  2.1 1.6 copy.9
  3.7 0.0 copy-done.2
  3.7 0.3 copy.10
  3.9 0.0 slice-start
  4.0 0.0 copy-start
  4.0 0.0 slice-start.1
  4.0 390.8 %ring_attention.1 = (f32[24,128,256]{2,1,0:T(8,128)S(1)}, f32[24,8,256]{2,1,0:T(8,128)S(1)}, bf16[24,128,256]{2,1,0:T(8,128)(2,1)}, bf16[16,4,8,256,128]{4,3,2,1...) custom-call(bf16[512,1536]{1,0:T(8,128)(2,1)} %x_ref.1, ...), custom_call_target="tpu_custom_call" | custom-call | tf_op jit(solution)/shard_map/ring_attention/pallas_call | solution.py:575
  394.8 0.0 slice-done
  394.8 0.0 copy-done
  394.8 0.0 slice-done.1
  394.8 5.3 %output.1 = bf16[512,1536]{1,0:T(8,128)(2,1)} custom-call(bf16[512,1536]{1,0:T(8,128)(2,1)S(1)} %copy-done, f32[24,128,256]{2,1,0:T(8,128)S(1)} %get-tuple-element.12.acc_ref, f32[24,8,256]{2,1,0:T(8,128)S(1)} %get-tuple-element.13.l_ref, bf16[1536,1536]{1,0:T(8,128)(2,1)S(1)} %bitcast.6, bf16[24,128,256]{2,1,0:T(8,128)(2,1)} %get-tuple-element.14.q_all, ...), custom_call_target="tpu_custom_call" | custom-call | tf_op jit(solution)/shard_map/output/pallas_call | solution.py:617
  (2 shorter events, 0.0 us)
Async XLA Ops:
  0.0 2.1 copy-start.1
  0.8 2.8 copy-start.2
  3.9 390.8 %slice-start = ((s8[4718592]{0:T(1024)(128)(4,1)}), s8[4194304]{0:T(1024)(128)(4,1)S(1)}, s32[]{:S(2)}) async-start(s8[4718592]{0:T(1024)(128)(4,1)} %bitcast.5), calls=%async_computation | async-start | bytes 8388608
  4.0 390.8 %copy-start = (bf16[512,1536]{1,0:T(8,128)(2,1)S(1)}, bf16[512,1536]{1,0:T(8,128)(2,1)}, u32[]{:S(2)}) copy-start(bf16[512,1536]{1,0:T(8,128)(2,1)} %x_ref.1) | copy-start | bytes 4718596
  4.0 390.8 %slice-start.1 = ((s8[4718592]{0:T(1024)(128)(4,1)}), s8[524288]{0:T(1024)(128)(4,1)S(1)}, s32[]{:S(2)}) async-start(s8[4718592]{0:T(1024)(128)(4,1)} %bitcast.5), calls=%async_computation.1 | async-start | bytes 1048576
